TPU v7x, 32 devices: a whole 2x2x4 slice. The times are simulated.
32 devices in a mesh: section: 2 (over core), dp: 8 (over z, x), tensor: 2 (over y).
Axes of the slice: x: 2, y: 2, z: 4, core: 2. Of those that a mesh axis runs over, the one named last changes fastest.
Arguments:
- tokens: bfloat16 [1024, 4096], P('dp', 'tensor'), may hold values from -6 to 6
- gain: bfloat16 [2, 4096], P('section', 'tensor'), may hold values from 0.099609375 to 1.8984375
- w_up: bfloat16 [2, 4096, 5120], P('section', 'dp', 'tensor'), may hold values from -0.09375 to 0.09375
- w_down: bfloat16 [2, 5120, 4096], P('section', 'tensor', 'dp'), may hold values from -0.078125 to 0.078125
- cotangent: bfloat16 [2, 1024, 4096], P('section', 'dp'), may hold values from -6 to 6
Outputs:
- states: bfloat16 [2, 1024, 4096], P('section', 'dp', 'tensor')
- grad_down: bfloat16 [2, 5120, 4096], P('section', 'tensor', 'dp')
All inputs are finite; a program needn't handle non-finite values.
Results may differ from a plain program's by a relative error of at most 0.02.
Values may be sent and summed in bfloat16 or wider, within the bound.
A program may use at most 128 MiB of HBM per device.

v0:
```python
import jax
import jax.numpy as jnp
from jax import lax
from jax.sharding import PartitionSpec as P

MICRO = 2
MB_ROWS = 64


EPS = 1e-06


def shifted(array, axis, by):
    peers = lax.axis_size(axis)
    pairs = [(i, i + by) for i in range(peers) if 0 <= i + by < peers]
    return lax.ppermute(array, axis, pairs)


def body(tokens, gain, w_up, w_down, cotangent):
    section_id = lax.axis_index("section")
    section_count = lax.axis_size("section")
    up_whole = lax.all_gather(w_up[0], "dp", axis=0, tiled=True)
    down_whole = lax.all_gather(w_down[0], "dp", axis=1, tiled=True)
    width = up_whole.shape[0]
    hidden_width = up_whole.shape[1]
    gain_own = gain[0]
    micro_rows = MB_ROWS
    micro_count = MICRO
    own_width = tokens.shape[1]
    tok_rows = tokens.shape[0]

    def project(normed):
        pre_act = jnp.dot(normed, up_whole, preferred_element_type=jnp.float32)
        hidden = jax.nn.gelu(pre_act, approximate=True).astype(jnp.bfloat16)
        partial_value = jnp.dot(hidden, down_whole, preferred_element_type=jnp.float32).astype(
            jnp.bfloat16
        )
        return (hidden, lax.optimization_barrier(partial_value).astype(jnp.float32))

    def skipped(normed):
        return (
            jnp.zeros((micro_rows, hidden_width), jnp.bfloat16),
            jnp.zeros((micro_rows, width), jnp.float32),
        )

    def advance(step_id, loop_state):
        incoming, states, hiddens = loop_state
        micro_id = step_id - section_id
        active = (micro_id >= 0) & (micro_id < micro_count)
        slot_pos = jnp.clip(micro_id, 0, micro_count - 1) * micro_rows
        entry_rows = lax.dynamic_slice_in_dim(tokens, slot_pos, micro_rows, 0)
        current = jnp.where(section_id == 0, entry_rows, incoming)
        current_f = current.astype(jnp.float32)
        own_sums = jnp.sum(current_f * current_f, axis=1)
        square_total = lax.psum(own_sums, "tensor")
        inverse_rms = lax.rsqrt(square_total / width + EPS)
        normed_own = (current_f * inverse_rms[:, None] * gain_own.astype(jnp.float32)).astype(
            jnp.bfloat16
        )
        normed = lax.all_gather(normed_own, "tensor", axis=1, tiled=True)
        hidden, partial_value = lax.cond(active, project, skipped, normed)
        summed = lax.psum_scatter(
            partial_value.astype(jnp.bfloat16), "tensor", scatter_dimension=1, tiled=True
        ).astype(jnp.float32)
        result = (current_f + summed).astype(jnp.bfloat16)
        old_state = lax.dynamic_slice_in_dim(states, slot_pos, micro_rows, 0)
        states = lax.dynamic_update_slice_in_dim(
            states, jnp.where(active, result, old_state), slot_pos, 0
        )
        old_hidden = lax.dynamic_slice_in_dim(hiddens, slot_pos, micro_rows, 0)
        hiddens = lax.dynamic_update_slice_in_dim(
            hiddens, jnp.where(active, hidden, old_hidden), slot_pos, 0
        )
        incoming = shifted(result, "section", 1)
        return (incoming, states, hiddens)

    initial = (
        jnp.zeros((micro_rows, own_width), jnp.bfloat16),
        jnp.zeros((tok_rows, own_width), jnp.bfloat16),
        jnp.zeros((tok_rows, hidden_width), jnp.bfloat16),
    )
    final_state = lax.fori_loop(0, micro_count + section_count - 1, advance, initial)
    states = final_state[1]
    hiddens = final_state[2]
    cot_own = cotangent[0]
    dp_count = lax.axis_size("dp")
    hidden_all = lax.all_gather(hiddens, "dp", axis=0, tiled=True)
    cot_mine = lax.all_to_all(cot_own, "dp", split_axis=1, concat_axis=0, tiled=True)
    grad_own = jnp.zeros((hidden_width, width // dp_count), jnp.float32)
    for peer_id in range(dp_count):
        lower = peer_id * tok_rows
        partial_value = lax.dot_general(
            hidden_all[lower : lower + tok_rows],
            cot_mine[lower : lower + tok_rows],
            (((0,), (0,)), ((), ())),
            preferred_element_type=jnp.float32,
        ).astype(jnp.bfloat16)
        grad_own = grad_own + lax.optimization_barrier(partial_value).astype(jnp.float32)
    return (states[None], grad_own.astype(jnp.bfloat16)[None])


def solution(mesh):
    placed = (
        P("dp", "tensor"),
        P("section", "tensor"),
        P("section", "dp", "tensor"),
        P("section", "tensor", "dp"),
        P("section", "dp", None),
    )
    return jax.shard_map(
        body,
        mesh=mesh,
        in_specs=placed,
        out_specs=(P("section", "dp", "tensor"), P("section", "tensor", "dp")),
        check_vma=False,
    )
```

profile of v0, /device:TPU:0, one launch (start us, length us, event | category | flops | bytes accessed | tf_op | source)
XLA Modules:
  0.0 1094.1 jit_solution(13235367819460651605)
XLA Ops:
  8.7 405.3 %all-gather.8.cloned.1.call-done = bf16[1,4096,2560]{2,1,0:T(8,128)(2,1)} async-done(((bf16[1,512,2560]{2,1,0:T(8,128)(2,1)}), bf16[1,4096,2560]{2,1,0:T(8,128)(2,1)}) %all-gather.8.cloned.1.call-update) | async-done | bytes 20971536 | tf_op jit(solution)/shard_map/all_gather | solution.py:22
  414.0 403.3 %all-gather.10.cloned.1.call-done = bf16[1,2560,4096]{2,1,0:T(8,128)(2,1)} async-done(((bf16[1,2560,512]{2,1,0:T(8,128)(2,1)}), bf16[1,2560,4096]{2,1,0:T(8,128)(2,1)}) %all-gather.10.cloned.1.call-update) | async-done | bytes 20971536 | tf_op jit(solution)/shard_map/all_gather | solution.py:23
  817.4 149.7 %while.18 = (s32[]{:T(128)}, bf16[64,2048]{1,0:T(8,128)(2,1)S(1)}, bf16[128,2048]{1,0:T(8,128)(2,1)S(1)}, bf16[128,2560]{1,0:T(8,128)(2,1)S(1)}, pred[]{:T(512)}...) while((s32[]{:T(128)}, bf16[64,2048]{1,0:T(8,128)(2,1)S(1)}, ...), condition=%wide.region_6.7_spmd, body=%wide.region_0.6_spmd.sunk | while | flops 2687961344 | bytes 137451440 | solution.py:82
  817.7 4.9 psum.13
  822.8 7.4 all_gather.21
  830.2 17.9 %conditional.2 = (bf16[64,2560]{1,0:T(8,128)(2,1)}, bf16[64,4096]{1,0:T(8,128)(2,1)S(1)}) conditional(s32[]{:T(128)} %convert_element_type.199, () %tuple.52, (bf16[64,4096]{1,0:T(8,128)(2,1)S(1)}, bf16[4096,2560]{1,0:T(8,128)(2,1)}, bf16[2560,4096]{1,0:T(8,128)(2,1)}) %tuple.53), branch_computations={%region_3.3_spmd, %region_4.4_spmd} | conditional | flops 2686091264 | bytes 127533096 | solution.py:61
  830.2 11.6 %fusion.7 = bf16[64,2560]{1,0:T(8,128)(2,1)} fusion(bf16[64,4096]{1,0:T(8,128)(2,1)S(1)} %get-tuple-element.189, bf16[4096,2560]{1,0:T(8,128)(2,1)} %get-tuple-element.190), kind=kOutput, calls=%fused_computation.9 | convolution fusion | flops 1343651840 | bytes 21823488 | tf_op jit(solution)/shard_map/while/body/eval_jaxpr/cond/branch_1_fun/dot_general | solution.py:33
  841.8 1.4 copy-done
  843.2 4.8 convolution_convert_fusion
  848.9 15.1 %reduce-scatter.2.cloned.1.call-done = bf16[64,2048]{1,0:T(8,128)(2,1)} async-done(((bf16[64,4096]{1,0:T(8,128)(2,1)}), bf16[64,2048]{1,0:T(8,128)(2,1)}) %reduce-scatter.2.cloned.1.call-update) | async-done | bytes 262160 | tf_op jit(solution)/shard_map/while/body/eval_jaxpr/reduce_scatter | solution.py:62
  864.0 1.1 select_dynamic-update-slice_fusion.4
  865.1 1.6 collective-permute-start
  866.7 1.1 select_dynamic-update-slice_fusion.5
  868.0 4.9 psum.13
  873.1 8.0 all_gather.21
  881.2 17.9 %conditional.2 = (bf16[64,2560]{1,0:T(8,128)(2,1)}, bf16[64,4096]{1,0:T(8,128)(2,1)S(1)}) conditional(s32[]{:T(128)} %convert_element_type.199, () %tuple.52, (bf16[64,4096]{1,0:T(8,128)(2,1)S(1)}, bf16[4096,2560]{1,0:T(8,128)(2,1)}, bf16[2560,4096]{1,0:T(8,128)(2,1)}) %tuple.53), branch_computations={%region_3.3_spmd, %region_4.4_spmd} | conditional | flops 2686091264 | bytes 127533096 | solution.py:61
  881.2 11.6 %fusion.7 = bf16[64,2560]{1,0:T(8,128)(2,1)} fusion(bf16[64,4096]{1,0:T(8,128)(2,1)S(1)} %get-tuple-element.189, bf16[4096,2560]{1,0:T(8,128)(2,1)} %get-tuple-element.190), kind=kOutput, calls=%fused_computation.9 | convolution fusion | flops 1343651840 | bytes 21823488 | tf_op jit(solution)/shard_map/while/body/eval_jaxpr/cond/branch_1_fun/dot_general | solution.py:33
  892.8 1.4 copy-done
  894.2 4.8 convolution_convert_fusion
  899.9 14.8 %reduce-scatter.2.cloned.1.call-done = bf16[64,2048]{1,0:T(8,128)(2,1)} async-done(((bf16[64,4096]{1,0:T(8,128)(2,1)}), bf16[64,2048]{1,0:T(8,128)(2,1)}) %reduce-scatter.2.cloned.1.call-update) | async-done | bytes 262160 | tf_op jit(solution)/shard_map/while/body/eval_jaxpr/reduce_scatter | solution.py:62
  915.7 1.6 collective-permute-start
  917.3 1.1 select_dynamic-update-slice_fusion.5
  918.7 4.9 psum.13
  923.8 8.0 all_gather.21
  933.5 29.8 %reduce-scatter.2.cloned.1.call-done = bf16[64,2048]{1,0:T(8,128)(2,1)} async-done(((bf16[64,4096]{1,0:T(8,128)(2,1)}), bf16[64,2048]{1,0:T(8,128)(2,1)}) %reduce-scatter.2.cloned.1.call-update) | async-done | bytes 262160 | tf_op jit(solution)/shard_map/while/body/eval_jaxpr/reduce_scatter | solution.py:62
  964.3 1.6 collective-permute-start
  967.9 1.6 copy.7
  969.6 51.9 %all_to_all.16 = bf16[128,8,512]{0,2,1:T(8,128)(2,1)S(1)} all-to-all(bf16[128,8,512]{0,2,1:T(8,128)(2,1)S(1)} %bitcast.46), channel_id=1, replica_groups=mesh['section'=2,'dp'=8,'tensor'=2] {'dp'}, dimensions={1} | all-to-all | bytes 2097152 | tf_op jit(solution)/shard_map/all_to_all | solution.py:88
  1021.4 52.5 %all-gather.6.cloned.1.call-done = bf16[1024,2560]{1,0:T(8,128)(2,1)} async-done(((bf16[128,2560]{1,0:T(8,128)(2,1)}), bf16[1024,2560]{1,0:T(8,128)(2,1)}) %all-gather.6.cloned.1.call-update) | async-done | bytes 5242896 | tf_op jit(solution)/shard_map/all_gather | solution.py:87
  1074.0 2.1 convolution_convert_fusion.1
  1076.1 2.0 convolution_convert_fusion.2
  1083.3 4.0 fusion.12
  (61 shorter events, 16.1 us)
Async XLA Ops:
  7.2 1.5 copy-start.6
  7.2 810.2 %copy-start.5 = (bf16[128,2048]{1,0:T(8,128)(2,1)S(1)}, bf16[128,2048]{1,0:T(8,128)(2,1)}, u32[]{:S(2)}) copy-start(bf16[128,2048]{1,0:T(8,128)(2,1)} %param.9) | copy-start | bytes 1572868
  7.2 406.8 %all-gather.8.cloned.1.call-start = ((), (), s32[]{:S(2)}) async-start(), calls=%async_computation.3 | async-start | bytes 23592960 | tf_op jit(solution)/shard_map/all_gather | solution.py:22
  7.9 809.3 %all-gather.10.cloned.1.call-start = ((), (), s32[]{:S(2)}) async-start(), calls=%async_computation.4 | async-start | bytes 23592960 | tf_op jit(solution)/shard_map/all_gather | solution.py:23
  817.4 46.6 %reduce-scatter.2.cloned.1.call-start = ((), (), s32[]{:S(2)}) async-start(), calls=%async_computation.5 | async-start | bytes 786432 | tf_op jit(solution)/shard_map/while/body/eval_jaxpr/reduce_scatter | solution.py:62
  830.2 13.0 %copy-start = (bf16[2560,4096]{1,0:T(8,128)(2,1)S(1)}, bf16[2560,4096]{1,0:T(8,128)(2,1)}, u32[]{:S(2)}) copy-start(bf16[2560,4096]{1,0:T(8,128)(2,1)} %get-tuple-element.191) | copy-start | bytes 62914564 | tf_op jit(solution)/shard_map/while/body/eval_jaxpr/cond
  848.1 0.8 copy-start.1
  865.1 2.7 collective-permute-start
  867.8 46.9 %reduce-scatter.2.cloned.1.call-start = ((), (), s32[]{:S(2)}) async-start(), calls=%async_computation.5 | async-start | bytes 786432 | tf_op jit(solution)/shard_map/while/body/eval_jaxpr/reduce_scatter | solution.py:62
  881.2 13.0 %copy-start = (bf16[2560,4096]{1,0:T(8,128)(2,1)S(1)}, bf16[2560,4096]{1,0:T(8,128)(2,1)}, u32[]{:S(2)}) copy-start(bf16[2560,4096]{1,0:T(8,128)(2,1)} %get-tuple-element.191) | copy-start | bytes 62914564 | tf_op jit(solution)/shard_map/while/body/eval_jaxpr/cond
  899.0 0.8 copy-start.1
  915.7 2.7 collective-permute-start
  918.5 44.8 %reduce-scatter.2.cloned.1.call-start = ((), (), s32[]{:S(2)}) async-start(), calls=%async_computation.5 | async-start | bytes 786432 | tf_op jit(solution)/shard_map/while/body/eval_jaxpr/reduce_scatter | solution.py:62
  932.6 0.8 copy-start.1
  964.3 2.7 collective-permute-start
  967.1 0.8 copy-start.2
  967.1 111.0 %copy-start.3 = (bf16[128,2048]{1,0:T(8,128)(2,1)}, bf16[128,2048]{1,0:T(8,128)(2,1)S(1)}, u32[]{:S(2)}) copy-start(bf16[128,2048]{1,0:T(8,128)(2,1)S(1)} %get-tuple-element.209) | copy-start | bytes 1572868
  967.1 106.9 %all-gather.6.cloned.1.call-start = ((), (), s32[]{:S(2)}) async-start(), calls=%async_computation.2 | async-start | bytes 5898240 | tf_op jit(solution)/shard_map/all_gather | solution.py:87
  1074.0 4.1 copy-start.4
Sparse Core Ops, SparseCore 0:
  9.5 404.4 all-gather.7
  415.5 401.6 all-gather.9
  849.0 14.9 reduce-scatter.1
  900.0 14.6 reduce-scatter.1
  933.6 29.6 reduce-scatter.1
  970.3 103.6 all-gather.5
where the time goes:
time: 1090 us
  waiting for transfers between devices  923 us (85%)
  blocking collectives  90.1 us (8%)
  matrix products  42.2 us (4%)
  between operations  14.2 us (1%)
    all_gather x1, waiting for transfers between devices, body(): up_whole = lax.all_gather(w_up[0], 'dp', axis=0, tiled=True)  405 us
    all_gather x1, waiting for transfers between devices, body(): down_whole = lax.all_gather(w_down[0], 'dp', axis=1, tiled=True)  403 us
    reduce_scatter x3, waiting for transfers between devices, advance(): lax.psum_scatter(partial_value.astype(jnp.bfloat16), 'tensor', scatter_di...  59.7 us
    all_gather x1, waiting for transfers between devices, body(): hidden_all = lax.all_gather(hiddens, 'dp', axis=0, tiled=True)  52.5 us
    all_to_all x1, blocking collectives, body(): lax.all_to_all(cot_own, 'dp', split_axis=1, concat_axis=0, tiled=True)  51.9 us
    all_gather x3, blocking collectives, advance(): normed = lax.all_gather(normed_own, 'tensor', axis=1, tiled=True)  23.5 us
    dot_general x2, matrix products, project(): pre_act = jnp.dot(normed, up_whole, preferred_element_type=jnp.float32)  23.3 us
  transfers between devices with their start and end apart: 9, of which 7 were waited for; matrix products, arithmetic and copies ran while one was open for 0% of the time, Pallas kernels for 0%

commit v1 on v0

v1 whole, which is shorter than its diff:
```python
import jax
import jax.numpy as jnp
from jax import lax
from jax.sharding import PartitionSpec as P

EPS = 1e-06
F32 = jnp.float32
BF16 = jnp.bfloat16


def body(tokens, gain, w_up, w_down, cotangent):
    core = lax.axis_index("section")
    layers = lax.axis_size("section")
    assert layers == 2
    dp_id = lax.axis_index("dp")
    dp_count = lax.axis_size("dp")
    tensor_id = lax.axis_index("tensor")
    tensor_count = lax.axis_size("tensor")
    rows, own_width = tokens.shape
    width = own_width * tensor_count
    slice_width = width // dp_count
    hidden_width = w_up.shape[2]
    half = hidden_width // layers
    other = 1 - core
    all_rows = rows * dp_count

    def swap(array):
        return lax.ppermute(array, "section", [(0, 1), (1, 0)])

    def both(own, got):
        return (jnp.where(core == 0, own, got), jnp.where(core == 0, got, own))

    cot_mine = lax.all_to_all(cotangent[0], "dp", split_axis=1, concat_axis=0, tiled=True)

    half_rows = rows // layers
    tok_half = lax.dynamic_slice_in_dim(tokens, core * half_rows, half_rows, 0)
    tok_full = lax.all_gather(tok_half, "tensor", axis=1, tiled=True)
    tok_f = tok_full.astype(F32)
    sums_half = jnp.sum(tok_f * tok_f, axis=1)
    sums_a, sums_b = both(sums_half, swap(sums_half))
    sums = jnp.concatenate([sums_a, sums_b])
    x_half = lax.all_to_all(tok_full, "dp", split_axis=1, concat_axis=0, tiled=True)
    x_a, x_b = both(x_half, swap(x_half))
    x = jnp.concatenate(
        [
            x_a.reshape(dp_count, half_rows, slice_width),
            x_b.reshape(dp_count, half_rows, slice_width),
        ],
        axis=1,
    ).reshape(all_rows, slice_width)

    gain_all = lax.all_gather(gain, "tensor", axis=1, tiled=True)
    gain_own = lax.dynamic_slice_in_dim(gain_all, dp_id * slice_width, slice_width, 1)
    gains = both(gain_own, swap(gain_own))

    up_parts = both(
        lax.dynamic_slice_in_dim(w_up[0], core * half, half, 1),
        swap(lax.dynamic_slice_in_dim(w_up[0], other * half, half, 1)),
    )
    down_parts = both(
        lax.dynamic_slice_in_dim(w_down[0], core * half, half, 0),
        swap(lax.dynamic_slice_in_dim(w_down[0], other * half, half, 0)),
    )

    states = []
    hiddens = []
    for layer in range(layers):
        x_f = x.astype(F32)
        if layer > 0:
            sums = lax.psum_scatter(
                jnp.sum(x_f * x_f, axis=1), "dp", scatter_dimension=0, tiled=True
            )
        scaled = (x_f * gains[layer].astype(F32)).astype(BF16)
        part = jnp.dot(scaled, up_parts[layer], preferred_element_type=F32).astype(BF16)
        pre = lax.psum_scatter(part, "dp", scatter_dimension=0, tiled=True)
        inverse_rms = lax.rsqrt(sums / width + EPS)
        hidden = jax.nn.gelu(pre.astype(F32) * inverse_rms[:, None], approximate=True).astype(BF16)
        hidden_all = lax.all_gather(hidden, "dp", axis=0, tiled=True)
        hiddens.append(hidden_all)
        out = jnp.dot(hidden_all, down_parts[layer], preferred_element_type=F32)
        mid = all_rows // layers
        keep = lax.dynamic_slice_in_dim(out, core * mid, mid, 0)
        give = lax.dynamic_slice_in_dim(out, other * mid, mid, 0).astype(BF16)
        summed = keep + swap(give).astype(F32)
        if tensor_count == 2:
            sent = summed.astype(BF16)
            got = lax.ppermute(sent, "tensor", [(0, 1), (1, 0)])
            summed = sent.astype(F32) + got.astype(F32)
        else:
            summed = lax.psum(summed.astype(BF16), "tensor").astype(F32)
        x_mid = lax.dynamic_slice_in_dim(x_f, core * mid, mid, 0)
        new_mid = (x_mid + summed).astype(BF16)
        new_a, new_b = both(new_mid, swap(new_mid))
        x = jnp.concatenate([new_a, new_b], axis=0)
        states.append(x)

    state_own = jnp.where(core == 0, states[0], states[1])
    state_rows = lax.all_to_all(state_own, "dp", split_axis=0, concat_axis=1, tiled=True)
    state = lax.dynamic_slice_in_dim(state_rows, tensor_id * own_width, own_width, 1)

    hid_keep = jnp.where(core == 0, hiddens[0], hiddens[1])
    hid_got = swap(jnp.where(core == 0, hiddens[1], hiddens[0]))
    hid_parts = both(hid_keep, hid_got)
    hidden_whole = jnp.concatenate(hid_parts, axis=1)
    grad = lax.dot_general(
        hidden_whole, cot_mine, (((0,), (0,)), ((), ())), preferred_element_type=F32
    ).astype(BF16)
    return (state[None], grad[None])


def solution(mesh):
    placed = (
        P("dp", "tensor"),
        P("section", "tensor"),
        P("section", "dp", "tensor"),
        P("section", "tensor", "dp"),
        P("section", "dp", None),
    )
    return jax.shard_map(
        body,
        mesh=mesh,
        in_specs=placed,
        out_specs=(P("section", "dp", "tensor"), P("section", "tensor", "dp")),
        check_vma=False,
    )
```

time: 1090 us -> 414 us (0.38)
  waiting for transfers between devices: 923 us -> 288 us
  blocking collectives: 90.1 us -> 33.8 us
  matrix products: 42.2 us -> 20 us
  starting transfers between devices: 4.93 us -> 20.3 us
  local copies, waits for them, and re-layouts: 8.55 us -> 22.6 us
    all_gather x3 -> x2, waiting for transfers between devices: 861 us -> 103 us  [body(): hidden_all = lax.all_gather(hidden, 'dp', axis=0, tiled=True)]
    reduce_scatter x3 -> x2, waiting for transfers between devices: 59.7 us -> 117 us  [body(): pre = lax.psum_scatter(part, 'dp', scatter_dimension=0, tiled=True)]
    all_to_all x1 -> x0, blocking collectives: 51.9 us -> none  [body(): lax.all_to_all(cot_own, 'dp', split_axis=1, concat_axis=0, tiled=True)]
    ppermute x3 -> x12, waiting for transfers between devices: 1.09 us -> 35.8 us  [the longest x2 24.6 us: body(): got = lax.ppermute(sent, 'tensor', [(0, 1), (1, 0)])]
    all_to_all x0 -> x3, waiting for transfers between devices: none -> 32.4 us  [the longest x1 16.5 us: body(): lax.all_to_all(state_own, 'dp', split_axis=0, concat_axis=1, tiled=True)]
    dot_general x12 -> x5, matrix products: 42.2 us -> 20 us  [the longest x2 7.84 us: body(): jnp.dot(scaled, up_parts[layer], preferred_element_type=F32).astype(BF16)]
    unnamed x0 -> x1, blocking collectives: none -> 19.5 us
    all_to_all x0 -> x3, starting transfers between devices: none -> 14.8 us  [the longest x1 6.16 us: body(): lax.all_to_all(tok_full, 'dp', split_axis=1, concat_axis=0, tiled=True)]
  transfers between devices with their start and end apart: 9 -> 19, of which waited for: 7 -> 15; matrix products, arithmetic and copies ran while one was open for 0% -> 6% of each run, Pallas kernels for 0% -> 0%
where the time goes in v1:
time: 414 us; the launch traced here: 413 us
  waiting for transfers between devices  288 us (70%)
  blocking collectives  33.8 us (8%)
  local copies, waits for them, and re-layouts  22.6 us (5%)
  starting transfers between devices  20.3 us (5%)
  matrix products  20 us (5%)
  between operations  14.7 us (4%)
  other arithmetic  14.5 us (4%)
    reduce_scatter x2, waiting for transfers between devices, body(): pre = lax.psum_scatter(part, 'dp', scatter_dimension=0, tiled=True)  117 us
    all_gather x2, waiting for transfers between devices, body(): hidden_all = lax.all_gather(hidden, 'dp', axis=0, tiled=True)  103 us
    ppermute x2, waiting for transfers between devices, body(): got = lax.ppermute(sent, 'tensor', [(0, 1), (1, 0)])  24.6 us
    unnamed x1, blocking collectives  19.5 us
    all_to_all x1, waiting for transfers between devices, body(): lax.all_to_all(state_own, 'dp', split_axis=0, concat_axis=1, tiled=True)  16.5 us
    ppermute x10, waiting for transfers between devices, swap(): return lax.ppermute(array, 'section', [(0, 1), (1, 0)])  11.3 us
    all_to_all x1, waiting for transfers between devices, body(): lax.all_to_all(tok_full, 'dp', split_axis=1, concat_axis=0, tiled=True)  11.2 us
    all_gather x1, blocking collectives, body(): tok_full = lax.all_gather(tok_half, 'tensor', axis=1, tiled=True)  9.97 us
  transfers between devices with their start and end apart: 19, of which 15 were waited for; matrix products, arithmetic and copies ran while one was open for 6% of the time, Pallas kernels for 0%

profile of v1, /device:TPU:0, one launch (start us, length us, event | category | flops | bytes accessed | tf_op | source)
XLA Modules:
  0.0 413.5 jit_solution(5616129061812105178)
XLA Ops:
  8.2 10.0 %all_gather.12 = bf16[64,4096]{1,0:T(8,128)(2,1)S(1)} all-gather(bf16[64,2048]{1,0:T(8,128)(2,1)S(1)} %constant_dynamic-slice_fusion.2), channel_id=1, replica_groups=mesh['section'=2,'dp'=8,'tensor'=2] {'tensor'}, dimensions={1}, use_global_device_ids=true | all-gather | bytes 786432 | tf_op jit(solution)/shard_map/all_gather | solution.py:37
  19.0 6.2 %all-to-all-start = ((bf16[64,8,512]{2,0,1:T(8,128)(2,1)}), bf16[64,8,512]{2,0,1:T(8,128)(2,1)S(1)}, u32[]{:S(2)}, u32[]{:S(2)}) async-start(bf16[64,8,512]{2,0,1:T(8,128)(2,1)} %bitcast.43), calls=%async_computation | async-start | bytes 1048576 | tf_op jit(solution)/shard_map/all_to_all | solution.py:42
  25.3 2.5 dynamic-slice_bitcast_fusion.1
  27.7 11.2 %all-to-all-done = bf16[64,8,512]{2,0,1:T(8,128)(2,1)S(1)} async-done(((bf16[64,8,512]{2,0,1:T(8,128)(2,1)}), bf16[64,8,512]{2,0,1:T(8,128)(2,1)S(1)}, u32[]{:S(2)}, u32[]{:S(2)}) %all-to-all-start) | async-done | bytes 524320 | tf_op jit(solution)/shard_map/all_to_all | solution.py:42
  38.9 4.3 %all_gather.13 = bf16[1,4096]{1,0:T(2,128)(2,1)S(1)} all-gather(bf16[1,2048]{1,0:T(2,128)(2,1)S(1)} %copy-done.12), channel_id=1, replica_groups=mesh['section'=2,'dp'=8,'tensor'=2] {'tensor'}, dimensions={1}, use_global_device_ids=true | all-gather | bytes 12288 | tf_op jit(solution)/shard_map/all_gather | solution.py:52
  46.4 3.1 convolution_convert_fusion.1
  52.2 68.8 %reduce-scatter.3.cloned.1.call-done = bf16[128,1280]{1,0:T(8,128)(2,1)} async-done(((bf16[1024,1280]{1,0:T(8,128)(2,1)}), bf16[128,1280]{1,0:T(8,128)(2,1)}) %reduce-scatter.3.cloned.1.call-update) | async-done | bytes 327696 | tf_op jit(solution)/shard_map/reduce_scatter | solution.py:75
  120.9 2.0 fusion.30
  123.0 2.5 dynamic-slice_bitcast_fusion
  125.5 3.4 collective-permute-done.4
  128.9 48.4 %all-gather.3.cloned.1.call-done = bf16[1024,1280]{1,0:T(8,128)(2,1)} async-done(((bf16[128,1280]{1,0:T(8,128)(2,1)}), bf16[1024,1280]{1,0:T(8,128)(2,1)}) %all-gather.3.cloned.1.call-update) | async-done | bytes 2621456 | tf_op jit(solution)/shard_map/all_gather | solution.py:78
  177.3 3.7 fusion.10
  183.1 2.1 collective-permute-done.5
  188.2 12.5 %collective-permute-done.6 = bf16[512,512]{1,0:T(8,128)(2,1)S(1)} collective-permute-done((bf16[512,512]{1,0:T(8,128)(2,1)S(1)}, bf16[512,512]{1,0:T(8,128)(2,1)S(1)}, u32[]{:S(2)}, u32[]{:S(2)}) %collective-permute-start.6) | collective-permute-done | bytes 524320 | tf_op jit(solution)/shard_map/ppermute | solution.py:87
  201.0 1.9 collective-permute-done.7
  203.0 4.8 %convolution_convert_fusion = bf16[1024,1280]{1,0:T(8,128)(2,1)} fusion(bf16[512,1280]{1,0:T(8,128)(2,1)} %collective-permute-done.2, pred[]{:T(512)S(6)} %eq.2, bf16[1,512,2560]{2,1,0:T(8,128)(2,1)S(1)} %copy-done.11, s32[]{:T(128)S(6)} %select_n.145, f32[512]{0:T(512)S(1)} %bitcast.52, bf16[512,512]{1,0:T(8,128)(2,1)S(1)} %get-tuple-element.7, ...), kind=kOutput, calls=%fused_computation.6 | convolution fusion | flops 1347289088 | bytes 6293509 | tf_op jit(solution)/shard_map/dot_general | solution.py:74
  209.9 19.5 %all-reduce = f32[1024]{0:T(1024)S(1)} all-reduce(f32[1024]{0:T(1024)S(1)} %multiply_reduce_fusion), channel_id=4, replica_groups=mesh['section'=2,'dp'=8,'tensor'=2] {'dp'}, use_global_device_ids=true, to_apply=%region_4.5.clone | all-reduce | flops 1024 | bytes 8192
  229.5 48.0 %reduce-scatter.5.cloned.1.call-done = bf16[128,1280]{1,0:T(8,128)(2,1)} async-done(((bf16[1024,1280]{1,0:T(8,128)(2,1)}), bf16[128,1280]{1,0:T(8,128)(2,1)}) %reduce-scatter.5.cloned.1.call-update) | async-done | bytes 327696 | tf_op jit(solution)/shard_map/reduce_scatter | solution.py:75
  277.5 2.0 fusion.38
  279.5 54.1 %all-gather.5.cloned.1.call-done = bf16[1024,1280]{1,0:T(8,128)(2,1)} async-done(((bf16[128,1280]{1,0:T(8,128)(2,1)}), bf16[1024,1280]{1,0:T(8,128)(2,1)}) %all-gather.5.cloned.1.call-update) | async-done | bytes 2621456 | tf_op jit(solution)/shard_map/all_gather | solution.py:78
  333.7 4.2 %fusion.11 = f32[1024,512]{1,0:T(8,128)S(1)} fusion(bf16[1024,1280]{1,0:T(8,128)(2,1)} %all-gather.5.cloned.1.call-done, bf16[1280,512]{1,0:T(8,128)(2,1)} %collective-permute-done.4, pred[]{:T(512)S(6)} %eq.2, bf16[1,2560,512]{2,1,0:T(8,128)(2,1)} %param.8, s32[]{:T(128)S(6)} %select_n.145), kind=kOutput, calls=%fused_computation.18 | convolution fusion | flops 1342832640 | bytes 7340037 | tf_op jit(solution)/shard_map/dot_general | solution.py:80
  342.4 2.3 copy.18
  344.7 4.2 %all-to-all-start.2 = ((bf16[128,8,512]{0,2,1:T(8,128)(2,1)}), bf16[128,8,512]{0,2,1:T(8,128)(2,1)}, u32[]{:S(2)}, u32[]{:S(2)}) async-start(bf16[128,8,512]{0,2,1:T(8,128)(2,1)} %bitcast.45), calls=%async_computation.4 | async-start | bytes 2097152 | tf_op jit(solution)/shard_map/all_to_all | solution.py:33
  352.4 12.1 %collective-permute-done.9 = bf16[512,512]{1,0:T(8,128)(2,1)S(1)} collective-permute-done((bf16[512,512]{1,0:T(8,128)(2,1)S(1)}, bf16[512,512]{1,0:T(8,128)(2,1)S(1)}, u32[]{:S(2)}, u32[]{:S(2)}) %collective-permute-start.9) | collective-permute-done | bytes 524320 | tf_op jit(solution)/shard_map/ppermute | solution.py:87
  364.8 1.9 collective-permute-done.10
  368.0 2.3 copy.16
  370.3 4.8 %all-to-all-done.2 = bf16[128,8,512]{0,2,1:T(8,128)(2,1)} async-done(((bf16[128,8,512]{0,2,1:T(8,128)(2,1)}), bf16[128,8,512]{0,2,1:T(8,128)(2,1)}, u32[]{:S(2)}, u32[]{:S(2)}) %all-to-all-start.2) | async-done | bytes 1048608 | tf_op jit(solution)/shard_map/all_to_all | solution.py:33
  375.1 4.4 %all-to-all-start.1 = ((bf16[8,128,512]{1,2,0:T(8,128)(2,1)}), bf16[8,128,512]{1,2,0:T(8,128)(2,1)}, u32[]{:S(2)}, u32[]{:S(2)}) async-start(bf16[8,128,512]{1,2,0:T(8,128)(2,1)} %copy.16), calls=%async_computation.3 | async-start | bytes 2097152 | tf_op jit(solution)/shard_map/all_to_all | solution.py:98
  379.6 2.3 copy.19
  381.8 2.3 broadcast_select_fusion.1
  384.1 4.3 %fusion.7 = bf16[1,2560,512]{2,1,0:T(8,128)(2,1)} fusion(bf16[1024,512]{1,0:T(8,128)(2,1)S(1)} %bitcast.50, bf16[1024,1280]{1,0:T(8,128)(2,1)S(1)} %get-tuple-element.3, bf16[1024,1280]{1,0:T(8,128)(2,1)S(1)} %get-tuple-element.2), kind=kOutput, calls=%fused_computation.5 | convolution fusion | flops 2696151040 | bytes 8912896 | tf_op jit(solution)/shard_map/dot_general | solution.py:105
  388.4 16.5 %all-to-all-done.1 = bf16[8,128,512]{1,2,0:T(8,128)(2,1)} async-done(((bf16[8,128,512]{1,2,0:T(8,128)(2,1)}), bf16[8,128,512]{1,2,0:T(8,128)(2,1)}, u32[]{:S(2)}, u32[]{:S(2)}) %all-to-all-start.1) | async-done | bytes 1048608 | tf_op jit(solution)/shard_map/all_to_all | solution.py:98
  (80 shorter events, 26.6 us)
Async XLA Ops:
  7.2 1.0 copy-start
  19.0 19.8 %copy-start.12 = (bf16[1,2048]{1,0:T(2,128)(2,1)S(1)}, bf16[1,2048]{1,0:T(2,128)(2,1)}, u32[]{:S(2)}) copy-start(bf16[1,2048]{1,0:T(2,128)(2,1)} %param.6) | copy-start | bytes 12292
  19.0 19.8 %all-to-all-start = ((bf16[64,8,512]{2,0,1:T(8,128)(2,1)}), bf16[64,8,512]{2,0,1:T(8,128)(2,1)S(1)}, u32[]{:S(2)}, u32[]{:S(2)}) async-start(bf16[64,8,512]{2,0,1:T(8,128)(2,1)} %bitcast.43), calls=%async_computation | async-start | bytes 1048576 | tf_op jit(solution)/shard_map/all_to_all | solution.py:42
  25.2 95.7 %reduce-scatter.3.cloned.1.call-start = ((), (), s32[]{:S(2)}) async-start(), calls=%async_computation.5 | async-start | bytes 2949120 | tf_op jit(solution)/shard_map/reduce_scatter | solution.py:75
  27.7 17.3 %collective-permute-start.2 = (bf16[512,1280]{1,0:T(8,128)(2,1)}, bf16[512,1280]{1,0:T(8,128)(2,1)}, u32[]{:S(2)}, u32[]{:S(2)}) collective-permute-start(bf16[512,1280]{1,0:T(8,128)(2,1)} %dynamic-slice_bitcast_fusion.1), channel_id=1, source_target_pairs={{0,16},{16,0},{1,17},{17,1},{2,18},{18,2},{3,19},{19,3},{4,20},{20... | collective-permute-start | bytes 3932168 | tf_op jit(solution)/shard_map/ppermute | solution.py:28
  38.9 5.6 %collective-permute-start = (bf16[512,512]{1,0:T(8,128)(2,1)S(1)}, bf16[512,512]{1,0:T(8,128)(2,1)S(1)}, u32[]{:S(2)}, u32[]{:S(2)}) collective-permute-start(bf16[512,512]{1,0:T(8,128)(2,1)S(1)} %bitcast.47), channel_id=1, source_target_pairs={{0,16},{16,0},{1,17},{17,1},{2,18},{18,2},{3,19},{19,3},{4,20},{20... | collective-permute-start | bytes 1572872 | tf_op jit(solution)/shard_map/ppermute | solution.py:28
  43.2 1.2 collective-permute-start.1
  44.6 1.7 copy-start.10
  49.5 127.8 %all-gather.3.cloned.1.call-start = ((), (), s32[]{:S(2)}) async-start(), calls=%async_computation.6 | async-start | bytes 2949120 | tf_op jit(solution)/shard_map/all_gather | solution.py:78
  49.7 2.3 collective-permute-start.3
  123.0 154.5 %reduce-scatter.5.cloned.1.call-start = ((), (), s32[]{:S(2)}) async-start(), calls=%async_computation.7 | async-start | bytes 2949120 | tf_op jit(solution)/shard_map/reduce_scatter | solution.py:75
  125.5 3.4 collective-permute-start.4
  180.9 1.3 copy-start.8
  183.1 2.1 collective-permute-start.5
  186.6 16.3 %copy-start.11 = (bf16[1,512,2560]{2,1,0:T(8,128)(2,1)S(1)}, bf16[1,512,2560]{2,1,0:T(8,128)(2,1)}, u32[]{:S(2)}) copy-start(bf16[1,512,2560]{2,1,0:T(8,128)(2,1)} %param.7) | copy-start | bytes 7864324
  186.7 14.0 %collective-permute-start.6 = (bf16[512,512]{1,0:T(8,128)(2,1)S(1)}, bf16[512,512]{1,0:T(8,128)(2,1)S(1)}, u32[]{:S(2)}, u32[]{:S(2)}) collective-permute-start(bf16[512,512]{1,0:T(8,128)(2,1)S(1)} %add_convert_fusion.3), channel_id=1, source_target_pairs={{0,1},{1,0},{2,3},{3,2},{4,5},{5,4},{6,7},{7,6},{8,9},{9,8},{10,11... | collective-permute-start | bytes 1572872 | tf_op jit(solution)/shard_map/ppermute | solution.py:87
  200.9 2.0 collective-permute-start.7
  203.0 6.7 %copy-start.3 = (bf16[512,512]{1,0:T(8,128)(2,1)}, bf16[512,512]{1,0:T(8,128)(2,1)S(1)}, u32[]{:S(2)}) copy-start(bf16[512,512]{1,0:T(8,128)(2,1)S(1)} %get-tuple-element.6) | copy-start | bytes 1572868
  203.0 6.7 %copy-start.5 = (bf16[512,512]{1,0:T(8,128)(2,1)}, bf16[512,512]{1,0:T(8,128)(2,1)S(1)}, u32[]{:S(2)}) copy-start(bf16[512,512]{1,0:T(8,128)(2,1)S(1)} %get-tuple-element.7) | copy-start | bytes 1572868
  207.8 125.9 %all-gather.5.cloned.1.call-start = ((), (), s32[]{:S(2)}) async-start(), calls=%async_computation.8 | async-start | bytes 2949120 | tf_op jit(solution)/shard_map/all_gather | solution.py:78
  333.6 6.4 %copy-start.1 = (bf16[1024,1280]{1,0:T(8,128)(2,1)S(1)}, bf16[1024,1280]{1,0:T(8,128)(2,1)}, u32[]{:S(2)}) copy-start(bf16[1024,1280]{1,0:T(8,128)(2,1)} %all-gather.3.cloned.1.call-done) | copy-start | bytes 7864324
  333.6 6.4 %copy-start.2 = (bf16[1024,1280]{1,0:T(8,128)(2,1)S(1)}, bf16[1024,1280]{1,0:T(8,128)(2,1)}, u32[]{:S(2)}) copy-start(bf16[1024,1280]{1,0:T(8,128)(2,1)} %all-gather.5.cloned.1.call-done) | copy-start | bytes 7864324
  337.8 1.3 copy-start.7
  340.0 8.9 %collective-permute-start.8 = (bf16[512,512]{1,0:T(8,128)(2,1)}, bf16[512,512]{1,0:T(8,128)(2,1)}, u32[]{:S(2)}, u32[]{:S(2)}) collective-permute-start(bf16[512,512]{1,0:T(8,128)(2,1)} %dynamic-slice_convert_fusion), channel_id=1, source_target_pairs={{0,16},{16,0},{1,17},{17,1},{2,18},{18,2},{3,19},{19,3},{4,20},{20... | collective-permute-start | bytes 1572872 | tf_op jit(solution)/shard_map/ppermute | solution.py:28
  341.9 40.0 %collective-permute-start.11 = (bf16[1024,1280]{1,0:T(8,128)(2,1)}, bf16[1024,1280]{1,0:T(8,128)(2,1)}, u32[]{:S(2)}, u32[]{:S(2)}) collective-permute-start(bf16[1024,1280]{1,0:T(8,128)(2,1)} %broadcast_select_fusion.2), channel_id=1, source_target_pairs={{0,16},{16,0},{1,17},{17,1},{2,18},{18,2},{3,19},{19,3},{4,20},{20... | collective-permute-start | bytes 7864328 | tf_op jit(solution)/shard_map/ppermute | solution.py:28
  344.7 30.5 %all-to-all-start.2 = ((bf16[128,8,512]{0,2,1:T(8,128)(2,1)}), bf16[128,8,512]{0,2,1:T(8,128)(2,1)}, u32[]{:S(2)}, u32[]{:S(2)}) async-start(bf16[128,8,512]{0,2,1:T(8,128)(2,1)} %bitcast.45), calls=%async_computation.4 | async-start | bytes 2097152 | tf_op jit(solution)/shard_map/all_to_all | solution.py:33
  348.9 3.2 copy-start.4
  348.9 3.2 copy-start.6
  350.6 13.9 %collective-permute-start.9 = (bf16[512,512]{1,0:T(8,128)(2,1)S(1)}, bf16[512,512]{1,0:T(8,128)(2,1)S(1)}, u32[]{:S(2)}, u32[]{:S(2)}) collective-permute-start(bf16[512,512]{1,0:T(8,128)(2,1)S(1)} %add_convert_fusion.1), channel_id=1, source_target_pairs={{0,1},{1,0},{2,3},{3,2},{4,5},{5,4},{6,7},{7,6},{8,9},{9,8},{10,11... | collective-permute-start | bytes 1572872 | tf_op jit(solution)/shard_map/ppermute | solution.py:87
  364.7 2.0 collective-permute-start.10
  375.1 29.8 %all-to-all-start.1 = ((bf16[8,128,512]{1,2,0:T(8,128)(2,1)}), bf16[8,128,512]{1,2,0:T(8,128)(2,1)}, u32[]{:S(2)}, u32[]{:S(2)}) async-start(bf16[8,128,512]{1,2,0:T(8,128)(2,1)} %copy.16), calls=%async_computation.3 | async-start | bytes 2097152 | tf_op jit(solution)/shard_map/all_to_all | solution.py:98
  381.8 2.3 copy-start.9
  (1 other events, 0.7 us)
Sparse Core Ops, SparseCore 0:
  49.6 71.2 reduce-scatter.2
  123.7 53.5 all-gather.2
  207.9 69.5 reduce-scatter.4
  280.1 53.4 all-gather.4

commit v2 on v1

--- a/solution.py
+++ b/solution.py
@@ -1,11 +1,284 @@
+import functools
+
 import jax
 import jax.numpy as jnp
 from jax import lax
+from jax.experimental import pallas as pl
+from jax.experimental.pallas import tpu as pltpu
 from jax.sharding import PartitionSpec as P
 
 EPS = 1e-06
 F32 = jnp.float32
 BF16 = jnp.bfloat16
+
+
+MESH = pl.DeviceIdType.MESH
+ROW_CHUNK = 16
+
+
+def far_first(count):
+    return sorted(range(1, count), key=lambda k: abs(2 * k - count)) + [0]
+
+
+def remote(src, dst, send_sem, recv_sem, target):
+    return pltpu.make_async_remote_copy(
+        src_ref=src,
+        dst_ref=dst,
+        send_sem=send_sem,
+        recv_sem=recv_sem,
+        device_id=target,
+        device_id_type=MESH,
+    )
+
+
+def layer_kernel(
+    dp_count,
+    inner,
+    width,
+    x_ref,
+    gain_ref,
+    up_ref,
+    hid_out,
+    scaled,
+    sum_send,
+    sum_recv,
+    x_send,
+    x_recv,
+    z_send,
+    z_recv,
+    total,
+    hid,
+    sum_ss,
+    sum_rs,
+    x_ss,
+    x_rs,
+    z_ss,
+    z_rs,
+    up_ss,
+    up_rs,
+    dn_ss,
+    dn_rs,
+    fx_ss,
+    fx_rs,
+    out_sem,
+):
+    outer = dp_count // inner
+    me = lax.axis_index("dp")
+    z = me // inner
+    x = lax.rem(me, inner)
+    peer = 1 - x
+    rows = x_ref.shape[1]
+
+    barrier = pltpu.get_barrier_semaphore()
+    for m in range(1, dp_count):
+        pl.semaphore_signal(
+            barrier, inc=1, device_id={"dp": lax.rem(me + m, dp_count)}, device_id_type=MESH
+        )
+    pl.semaphore_wait(barrier, dp_count - 1)
+
+    row_id = lax.broadcasted_iota(jnp.int32, (rows, rows), 0)
+    col_id = lax.broadcasted_iota(jnp.int32, (rows, rows), 1)
+    eye = row_id == col_id
+    gain_f = gain_ref[...].astype(F32)
+
+    def prepare(block, _):
+        values = x_ref[block].astype(F32)
+        scaled[block] = (values * gain_f).astype(BF16)
+        column = jnp.sum(values * values, axis=1, keepdims=True)
+        sum_send[block] = jnp.sum(jnp.where(eye, column, 0.0), axis=0, keepdims=True)
+        return 0
+
+    lax.fori_loop(0, dp_count, prepare, 0)
+
+    order = far_first(outer)
+    x_copies = {}
+    for k in order:
+        zz = lax.rem(z + k, outer)
+        x_send[k] = jnp.dot(
+            scaled[zz * inner + peer], up_ref[...], preferred_element_type=F32
+        ).astype(BF16)
+        x_copies[k] = remote(
+            x_send.at[k], x_recv.at[k], x_ss.at[k], x_rs.at[k], {"dp": z * inner + peer}
+        )
+        x_copies[k].start()
+    sum_copies = []
+    for m in range(1, dp_count):
+        target = lax.rem(me + m, dp_count)
+        copy = remote(
+            sum_send.at[target], sum_recv.at[m], sum_ss.at[m], sum_rs.at[m], {"dp": target}
+        )
+        copy.start()
+        sum_copies.append(copy)
+    z_copies = {}
+    for k in order:
+        zz = lax.rem(z + k, outer)
+        mine = jnp.dot(scaled[zz * inner + x], up_ref[...], preferred_element_type=F32)
+        x_copies[k].wait_recv()
+        if k == 0:
+            total[...] = mine + x_recv[k].astype(F32)
+        else:
+            z_send[k] = (mine + x_recv[k].astype(F32)).astype(BF16)
+            z_copies[k] = remote(
+                z_send.at[k], z_recv.at[k], z_ss.at[k], z_rs.at[k], {"dp": zz * inner + x}
+            )
+            z_copies[k].start()
+    sums = sum_send[me]
+    for m in range(1, dp_count):
+        sum_copies[m - 1].wait_recv()
+        sums = sums + sum_recv[m]
+    inverse = lax.rsqrt(jnp.sum(jnp.where(eye, sums, 0.0), axis=1, keepdims=True) / width + EPS)
+    for k in order[:-1]:
+        z_copies[k].wait_recv()
+
+    for lower in range(0, rows, ROW_CHUNK):
+        rows_now = pl.ds(lower, ROW_CHUNK)
+        value = total[rows_now]
+        for k in order[:-1]:
+            value = value + z_recv[k, rows_now].astype(F32)
+        value = value * inverse[lower : lower + ROW_CHUNK]
+        hid[me, rows_now] = jax.nn.gelu(value, approximate=True).astype(BF16)
+
+    def forward(origin, sem_id):
+        return remote(
+            hid.at[origin * inner + x],
+            hid.at[origin * inner + x],
+            fx_ss.at[sem_id],
+            fx_rs.at[sem_id],
+            {"dp": z * inner + peer},
+        )
+
+    def expect(origin, sem_id):
+        return remote(
+            hid.at[origin * inner + peer],
+            hid.at[origin * inner + peer],
+            fx_ss.at[sem_id],
+            fx_rs.at[sem_id],
+            {"dp": z * inner + peer},
+        )
+
+    def hop(origin, target, sends, recvs, j):
+        return remote(
+            hid.at[origin * inner + x],
+            hid.at[origin * inner + x],
+            sends.at[j],
+            recvs.at[j],
+            {"dp": target * inner + x},
+        )
+
+    def landing(origin, sends, recvs, j):
+        return remote(
+            hid.at[origin * inner + x],
+            hid.at[origin * inner + x],
+            sends.at[j],
+            recvs.at[j],
+            {"dp": z * inner + peer},
+        )
+
+    def store(block):
+        return pltpu.make_async_copy(hid.at[block], hid_out.at[block], out_sem.at[block])
+
+    last = outer - 1
+    for j in range(outer):
+        if j < last:
+
+            @pl.when((z - j >= 0) & (z < last))
+            def _():
+                hop(z - j, z + 1, up_ss, up_rs, j).start()
+
+            @pl.when((z + j <= last) & (z > 0))
+            def _():
+                hop(z + j, z - 1, dn_ss, dn_rs, j).start()
+
+        if j == 0:
+            forward(z, 0).start()
+            store(me).start()
+        if j < last:
+
+            @pl.when(z - 1 - j >= 0)
+            def _():
+                landing(z - 1 - j, up_ss, up_rs, j).wait_recv()
+                forward(z - 1 - j, 1 + j).start()
+                store((z - 1 - j) * inner + x).start()
+
+            @pl.when(z + 1 + j <= last)
+            def _():
+                landing(z + 1 + j, dn_ss, dn_rs, j).wait_recv()
+                forward(z + 1 + j, outer + j).start()
+                store((z + 1 + j) * inner + x).start()
+
+    expect(z, 0).wait_recv()
+    store(z * inner + peer).start()
+    for j in range(last):
+
+        @pl.when(z - 1 - j >= 0)
+        def _():
+            expect(z - 1 - j, 1 + j).wait_recv()
+            store((z - 1 - j) * inner + peer).start()
+
+        @pl.when(z + 1 + j <= last)
+        def _():
+            expect(z + 1 + j, outer + j).wait_recv()
+            store((z + 1 + j) * inner + peer).start()
+
+    for copy in list(x_copies.values()) + list(z_copies.values()) + sum_copies:
+        copy.wait_send()
+    forward(z, 0).wait_send()
+    for j in range(last):
+
+        @pl.when((z - j >= 0) & (z < last))
+        def _():
+            hop(z - j, z + 1, up_ss, up_rs, j).wait_send()
+
+        @pl.when((z + j <= last) & (z > 0))
+        def _():
+            hop(z + j, z - 1, dn_ss, dn_rs, j).wait_send()
+
+        @pl.when(z - 1 - j >= 0)
+        def _():
+            forward(z - 1 - j, 1 + j).wait_send()
+
+        @pl.when(z + 1 + j <= last)
+        def _():
+            forward(z + 1 + j, outer + j).wait_send()
+
+    for block in range(dp_count):
+        store(block).wait()
+
+
+def layer_hidden(layer, dp_count, width, x, gain_row, up):
+    rows = x.shape[0] // dp_count
+    slice_width = x.shape[1]
+    half = up.shape[1]
+    inner = 2
+    assert dp_count % inner == 0
+    outer = dp_count // inner
+    dma = pltpu.SemaphoreType.DMA
+    vmem = pl.BlockSpec(memory_space=pltpu.VMEM)
+    wide = pltpu.VMEM((outer, rows, half), BF16)
+    hidden = pl.pallas_call(
+        functools.partial(layer_kernel, dp_count, inner, width),
+        name=f"layer{layer}",
+        out_shape=jax.ShapeDtypeStruct((dp_count, rows, half), BF16),
+        in_specs=[vmem] * 3,
+        out_specs=pl.BlockSpec(memory_space=pl.ANY),
+        scratch_shapes=[
+            pltpu.VMEM((dp_count, rows, slice_width), BF16),
+            pltpu.VMEM((dp_count, 1, rows), F32),
+            pltpu.VMEM((dp_count, 1, rows), F32),
+            wide,
+            wide,
+            wide,
+            wide,
+            pltpu.VMEM((rows, half), F32),
+            pltpu.VMEM((dp_count, rows, half), BF16),
+        ]
+        + [dma((dp_count,))] * 2
+        + [dma((outer,))] * 8
+        + [dma((2 * outer,))] * 2
+        + [dma((dp_count,))],
+        compiler_params=pltpu.CompilerParams(collective_id=layer, has_side_effects=True),
+    )(x.reshape(dp_count, rows, slice_width), gain_row, up)
+    return hidden.reshape(dp_count * rows, half)
 
 
 def body(tokens, gain, w_up, w_down, cotangent):
@@ -35,10 +308,6 @@
     half_rows = rows // layers
     tok_half = lax.dynamic_slice_in_dim(tokens, core * half_rows, half_rows, 0)
     tok_full = lax.all_gather(tok_half, "tensor", axis=1, tiled=True)
-    tok_f = tok_full.astype(F32)
-    sums_half = jnp.sum(tok_f * tok_f, axis=1)
-    sums_a, sums_b = both(sums_half, swap(sums_half))
-    sums = jnp.concatenate([sums_a, sums_b])
     x_half = lax.all_to_all(tok_full, "dp", split_axis=1, concat_axis=0, tiled=True)
     x_a, x_b = both(x_half, swap(x_half))
     x = jnp.concatenate(
@@ -66,16 +335,7 @@
     hiddens = []
     for layer in range(layers):
         x_f = x.astype(F32)
-        if layer > 0:
-            sums = lax.psum_scatter(
-                jnp.sum(x_f * x_f, axis=1), "dp", scatter_dimension=0, tiled=True
-            )
-        scaled = (x_f * gains[layer].astype(F32)).astype(BF16)
-        part = jnp.dot(scaled, up_parts[layer], preferred_element_type=F32).astype(BF16)
-        pre = lax.psum_scatter(part, "dp", scatter_dimension=0, tiled=True)
-        inverse_rms = lax.rsqrt(sums / width + EPS)
-        hidden = jax.nn.gelu(pre.astype(F32) * inverse_rms[:, None], approximate=True).astype(BF16)
-        hidden_all = lax.all_gather(hidden, "dp", axis=0, tiled=True)
+        hidden_all = layer_hidden(layer, dp_count, width, x, gains[layer], up_parts[layer])
         hiddens.append(hidden_all)
         out = jnp.dot(hidden_all, down_parts[layer], preferred_element_type=F32)
         mid = all_rows // layers

time: 414 us -> 298 us (0.72)
  waiting for transfers between devices: 288 us -> 61.6 us
  Pallas kernels: 0 us -> 156 us
  blocking collectives: 33.8 us -> 14.6 us
  between operations: 14.7 us -> 0.95 us
  matrix products: 20 us -> 11.8 us
  local copies, waits for them, and re-layouts: 22.6 us -> 15.4 us
    pallas_call x0 -> x2, Pallas kernels: none -> 156 us  [layer_hidden(): pl.pallas_call(functools.partial(layer_kernel, dp_count, inner, width), n...]
    reduce_scatter x2 -> x0, waiting for transfers between devices: 117 us -> none  [body(): pre = lax.psum_scatter(part, 'dp', scatter_dimension=0, tiled=True)]
    all_gather x2 -> x0, waiting for transfers between devices: 103 us -> none  [body(): hidden_all = lax.all_gather(hidden, 'dp', axis=0, tiled=True)]
    unnamed x1 -> x0, blocking collectives: 19.5 us -> none
    all_to_all x1, waiting for transfers between devices: 4.83 us -> 14.7 us  [body(): lax.all_to_all(cotangent[0], 'dp', split_axis=1, concat_axis=0, tiled=True)]
    dot_general x2 -> x0, matrix products: 7.84 us -> none  [body(): jnp.dot(scaled, up_parts[layer], preferred_element_type=F32).astype(BF16)]
    ppermute x2, waiting for transfers between devices: 24.6 us -> 18.4 us  [body(): got = lax.ppermute(sent, 'tensor', [(0, 1), (1, 0)])]
    select_n x5 -> x6, other arithmetic: 2.54 us -> 8.28 us  [both(): return (jnp.where(core == 0, own, got), jnp.where(core == 0, got, own))]
  transfers between devices with their start and end apart: 19 -> 14, of which waited for: 15 -> 9; matrix products, arithmetic and copies ran while one was open for 6% -> 9% of each run, Pallas kernels for 0% -> 27%
where the time goes in v2:
time: 298 us; the launch traced here: 297 us
  Pallas kernels  156 us (52%)
  waiting for transfers between devices  61.6 us (21%)
  starting transfers between devices  19.1 us (6%)
  other arithmetic  18 us (6%)
  local copies, waits for them, and re-layouts  15.4 us (5%)
  blocking collectives  14.6 us (5%)
  matrix products  11.8 us (4%)
    pallas_call x2, Pallas kernels, layer_hidden(): pl.pallas_call(functools.partial(layer_kernel, dp_count, inner, width), n...  156 us
    ppermute x2, waiting for transfers between devices, body(): got = lax.ppermute(sent, 'tensor', [(0, 1), (1, 0)])  18.4 us
    all_to_all x1, waiting for transfers between devices, body(): lax.all_to_all(state_own, 'dp', split_axis=0, concat_axis=1, tiled=True)  15.9 us
    all_to_all x1, waiting for transfers between devices, body(): lax.all_to_all(cotangent[0], 'dp', split_axis=1, concat_axis=0, tiled=True)  14.7 us
    all_gather x1, blocking collectives, body(): tok_full = lax.all_gather(tok_half, 'tensor', axis=1, tiled=True)  10.3 us
    select_n x6, other arithmetic, both(): return (jnp.where(core == 0, own, got), jnp.where(core == 0, got, own))  8.28 us
    dot_general x2, matrix products, body(): out = jnp.dot(hidden_all, down_parts[layer], preferred_element_type=F32)  7.49 us
    ppermute x9, waiting for transfers between devices, swap(): return lax.ppermute(array, 'section', [(0, 1), (1, 0)])  6.84 us
  transfers between devices with their start and end apart: 14, of which 9 were waited for; matrix products, arithmetic and copies ran while one was open for 9% of the time, Pallas kernels for 27%

profile of v2, /device:TPU:0, one launch (start us, length us, event | category | flops | bytes accessed | tf_op | source)
XLA Modules:
  0.0 297.3 jit_solution(17403293083935005831)
XLA Ops:
  0.7 2.5 dynamic-slice_bitcast_fusion.1
  3.7 10.3 %all_gather.6 = bf16[64,4096]{1,0:T(8,128)(2,1)S(1)} all-gather(bf16[64,2048]{1,0:T(8,128)(2,1)S(1)} %constant_dynamic-slice_fusion.2), channel_id=1, replica_groups=mesh['section'=2,'dp'=8,'tensor'=2] {'tensor'}, dimensions={1}, use_global_device_ids=true | all-gather | bytes 786432 | tf_op jit(solution)/shard_map/all_gather | solution.py:310
  14.8 6.0 %all-to-all-start = ((bf16[64,8,512]{2,0,1:T(8,128)(2,1)}), bf16[64,8,512]{2,0,1:T(8,128)(2,1)}, u32[]{:S(2)}, u32[]{:S(2)}) async-start(bf16[64,8,512]{2,0,1:T(8,128)(2,1)} %bitcast.54), calls=%async_computation | async-start | bytes 1048576 | tf_op jit(solution)/shard_map/all_to_all | solution.py:311
  20.9 2.5 dynamic-slice_bitcast_fusion
  23.3 4.3 %all_gather.7 = bf16[1,4096]{1,0:T(2,128)(2,1)S(1)} all-gather(bf16[1,2048]{1,0:T(2,128)(2,1)S(1)} %copy-done.11), channel_id=1, replica_groups=mesh['section'=2,'dp'=8,'tensor'=2] {'tensor'}, dimensions={1}, use_global_device_ids=true | all-gather | bytes 12288 | tf_op jit(solution)/shard_map/all_gather | solution.py:321
  29.5 5.8 %all-to-all-done = bf16[64,8,512]{2,0,1:T(8,128)(2,1)} async-done(((bf16[64,8,512]{2,0,1:T(8,128)(2,1)}), bf16[64,8,512]{2,0,1:T(8,128)(2,1)}, u32[]{:S(2)}, u32[]{:S(2)}) %all-to-all-start) | async-done | bytes 524320 | tf_op jit(solution)/shard_map/all_to_all | solution.py:311
  35.3 3.3 %bitcast_select_fusion.4 = (bf16[512,1280]{1,0:T(8,128)(2,1)}, bf16[512,1280]{1,0:T(8,128)(2,1)}) fusion(bf16[512,1280]{1,0:T(8,128)(2,1)} %collective-permute-done.2, pred[]{:T(512)S(6)} %eq.2, bf16[1,512,2560]{2,1,0:T(8,128)(2,1)S(1)} %copy-done.7, s32[]{:T(128)S(6)} %select_n.130), kind=kLoop, calls=%fused_computation.14 | loop fusion | flops 1310720 | bytes 5242885 | tf_op jit(solution)/shard_map/jit(_where)/select_n | solution.py:304
  38.6 1.2 broadcast_select_fusion.10
  40.8 78.8 %layer0.1 = bf16[8,128,1280]{2,1,0:T(8,128)(2,1)} custom-call(bf16[8,128,512]{2,1,0:T(8,128)(2,1)} %pad_maximum_fusion.1.x_ref, bf16[1,512]{1,0:T(2,128)(2,1)} %get-tuple-element.13.gain_ref, bf16[512,1280]{1,0:T(8,128)(2,1)} %get-tuple-element.5.up_ref), custom_call_target="tpu_custom_call" | custom-call | tf_op jit(solution)/shard_map/layer0/pallas_call | solution.py:258
  119.6 3.3 %fusion.10 = f32[1024,512]{1,0:T(8,128)S(1)} fusion(bf16[1024,1280]{1,0:T(8,128)(2,1)} %bitcast.46, bf16[1280,512]{1,0:T(8,128)(2,1)} %collective-permute-done.3, pred[]{:T(512)S(6)} %eq.2, bf16[1,2560,512]{2,1,0:T(8,128)(2,1)S(1)} %copy-done.10, s32[]{:T(128)S(6)} %select_n.130), kind=kOutput, calls=%fused_computation.12 | convolution fusion | flops 1342832640 | bytes 7340037 | tf_op jit(solution)/shard_map/dot_general | solution.py:340
  122.9 1.3 copy-done.8
  124.4 1.9 collective-permute-done.4
  126.3 1.4 add_convert_fusion.2
  127.7 1.6 collective-permute-start.5
  129.3 12.5 %collective-permute-done.5 = bf16[512,512]{1,0:T(8,128)(2,1)S(1)} collective-permute-done((bf16[512,512]{1,0:T(8,128)(2,1)S(1)}, bf16[512,512]{1,0:T(8,128)(2,1)S(1)}, u32[]{:S(2)}, u32[]{:S(2)}) %collective-permute-start.5) | collective-permute-done | bytes 524320 | tf_op jit(solution)/shard_map/ppermute | solution.py:347
  142.0 1.9 collective-permute-done.6
  145.8 77.0 %layer1.1 = bf16[8,128,1280]{2,1,0:T(8,128)(2,1)} custom-call(bf16[8,128,512]{2,1,0:T(8,128)(2,1)} %bitcast.48, bf16[1,512]{1,0:T(2,128)(2,1)} %get-tuple-element.12.gain_ref, bf16[512,1280]{1,0:T(8,128)(2,1)} %get-tuple-element.4.up_ref), custom_call_target="tpu_custom_call" | custom-call | tf_op jit(solution)/shard_map/layer1/pallas_call | solution.py:258
  222.9 4.2 %fusion.11 = f32[1024,512]{1,0:T(8,128)S(1)} fusion(bf16[1024,1280]{1,0:T(8,128)(2,1)} %bitcast.47, bf16[1280,512]{1,0:T(8,128)(2,1)} %collective-permute-done.3, pred[]{:T(512)S(6)} %eq.2, bf16[1,2560,512]{2,1,0:T(8,128)(2,1)} %param.8, s32[]{:T(128)S(6)} %select_n.130), kind=kOutput, calls=%fused_computation.13 | convolution fusion | flops 1342832640 | bytes 7340037 | tf_op jit(solution)/shard_map/dot_general | solution.py:340
  227.3 2.1 broadcast_select_fusion.2
  230.8 1.5 collective-permute-start.8
  232.3 2.3 copy.13
  234.6 4.4 %all-to-all-start.2 = ((bf16[128,8,512]{0,2,1:T(8,128)(2,1)}), bf16[128,8,512]{0,2,1:T(8,128)(2,1)}, u32[]{:S(2)}, u32[]{:S(2)}) async-start(bf16[128,8,512]{0,2,1:T(8,128)(2,1)} %bitcast.51), calls=%async_computation.2 | async-start | bytes 2097152 | tf_op jit(solution)/shard_map/all_to_all | solution.py:306
  239.1 6.0 %collective-permute-done.8 = bf16[512,512]{1,0:T(8,128)(2,1)} collective-permute-done((bf16[512,512]{1,0:T(8,128)(2,1)}, bf16[512,512]{1,0:T(8,128)(2,1)}, u32[]{:S(2)}, u32[]{:S(2)}) %collective-permute-start.8) | collective-permute-done | bytes 524320 | tf_op jit(solution)/shard_map/ppermute | solution.py:347
  245.0 1.9 add_convert_fusion
  246.9 1.9 collective-permute-done.9
  250.1 14.7 %all-to-all-done.2 = bf16[128,8,512]{0,2,1:T(8,128)(2,1)} async-done(((bf16[128,8,512]{0,2,1:T(8,128)(2,1)}), bf16[128,8,512]{0,2,1:T(8,128)(2,1)}, u32[]{:S(2)}, u32[]{:S(2)}) %all-to-all-start.2) | async-done | bytes 1048608 | tf_op jit(solution)/shard_map/all_to_all | solution.py:306
  264.8 4.3 %all-to-all-start.1 = ((bf16[8,128,512]{2,1,0:T(8,128)(2,1)}), bf16[8,128,512]{2,1,0:T(8,128)(2,1)}, u32[]{:S(2)}, u32[]{:S(2)}) async-start(bf16[8,128,512]{2,1,0:T(8,128)(2,1)} %broadcast_select_fusion.4), calls=%async_computation.1 | async-start | bytes 2097152 | tf_op jit(solution)/shard_map/all_to_all | solution.py:358
  269.1 2.3 copy.14
  271.4 3.1 %broadcast_select_fusion.1 = (bf16[1024,1280]{1,0:T(8,128)(2,1)S(1)}, bf16[1024,1280]{1,0:T(8,128)(2,1)S(1)}) fusion(bf16[1024,1280]{1,0:T(8,128)(2,1)} %collective-permute-done.10, pred[]{:T(512)S(6)} %eq.2, bf16[8,128,1280]{2,1,0:T(8,128)(2,1)} %layer1.1, bf16[8,128,1280]{2,1,0:T(8,128)(2,1)S(1)} %copy-done.1), kind=kLoop, calls=%fused_computation.7 | loop fusion | flops 3932160 | bytes 13107201 | tf_op jit(solution)/shard_map/jit(_where)/select_n | solution.py:304
  274.5 4.3 %fusion.7 = bf16[1,2560,512]{2,1,0:T(8,128)(2,1)} fusion(bf16[1024,512]{1,0:T(8,128)(2,1)S(1)} %bitcast.58, bf16[1024,1280]{1,0:T(8,128)(2,1)S(1)} %get-tuple-element.3, bf16[1024,1280]{1,0:T(8,128)(2,1)S(1)} %get-tuple-element.2), kind=kOutput, calls=%fused_computation.5 | convolution fusion | flops 2696151040 | bytes 8912896 | tf_op jit(solution)/shard_map/dot_general | solution.py:365
  278.7 15.9 %all-to-all-done.1 = bf16[8,128,512]{2,1,0:T(8,128)(2,1)} async-done(((bf16[8,128,512]{2,1,0:T(8,128)(2,1)}), bf16[8,128,512]{2,1,0:T(8,128)(2,1)}, u32[]{:S(2)}, u32[]{:S(2)}) %all-to-all-start.1) | async-done | bytes 1048608 | tf_op jit(solution)/shard_map/all_to_all | solution.py:358
  294.7 1.6 copy.11
  (54 shorter events, 10.5 us)
Async XLA Ops:
  0.6 3.0 %copy-start = (bf16[128,2048]{1,0:T(8,128)(2,1)S(1)}, bf16[128,2048]{1,0:T(8,128)(2,1)}, u32[]{:S(2)}) copy-start(bf16[128,2048]{1,0:T(8,128)(2,1)} %param.5) | copy-start | bytes 1572868
  3.2 32.1 %collective-permute-start.2 = (bf16[512,1280]{1,0:T(8,128)(2,1)}, bf16[512,1280]{1,0:T(8,128)(2,1)}, u32[]{:S(2)}, u32[]{:S(2)}) collective-permute-start(bf16[512,1280]{1,0:T(8,128)(2,1)} %dynamic-slice_bitcast_fusion.1), channel_id=1, source_target_pairs={{0,16},{16,0},{1,17},{17,1},{2,18},{18,2},{3,19},{19,3},{4,20},{20... | collective-permute-start | bytes 3932168 | tf_op jit(solution)/shard_map/ppermute | solution.py:301
  3.7 19.7 %copy-start.11 = (bf16[1,2048]{1,0:T(2,128)(2,1)S(1)}, bf16[1,2048]{1,0:T(2,128)(2,1)}, u32[]{:S(2)}) copy-start(bf16[1,2048]{1,0:T(2,128)(2,1)} %param.6) | copy-start | bytes 12292
  3.7 31.6 %copy-start.7 = (bf16[1,512,2560]{2,1,0:T(8,128)(2,1)S(1)}, bf16[1,512,2560]{2,1,0:T(8,128)(2,1)}, u32[]{:S(2)}) copy-start(bf16[1,512,2560]{2,1,0:T(8,128)(2,1)} %param.7) | copy-start | bytes 7864324
  14.8 20.4 %all-to-all-start = ((bf16[64,8,512]{2,0,1:T(8,128)(2,1)}), bf16[64,8,512]{2,0,1:T(8,128)(2,1)}, u32[]{:S(2)}, u32[]{:S(2)}) async-start(bf16[64,8,512]{2,0,1:T(8,128)(2,1)} %bitcast.54), calls=%async_computation | async-start | bytes 1048576 | tf_op jit(solution)/shard_map/all_to_all | solution.py:311
  23.3 96.3 %collective-permute-start.3 = (bf16[1280,512]{1,0:T(8,128)(2,1)}, bf16[1280,512]{1,0:T(8,128)(2,1)}, u32[]{:S(2)}, u32[]{:S(2)}) collective-permute-start(bf16[1280,512]{1,0:T(8,128)(2,1)} %dynamic-slice_bitcast_fusion), channel_id=1, source_target_pairs={{0,16},{16,0},{1,17},{17,1},{2,18},{18,2},{3,19},{19,3},{4,20},{20... | collective-permute-start | bytes 3932168 | tf_op jit(solution)/shard_map/ppermute | solution.py:301
  27.7 1.2 collective-permute-start.1
  35.3 3.3 %collective-permute-start = (bf16[512,512]{1,0:T(8,128)(2,1)}, bf16[512,512]{1,0:T(8,128)(2,1)S(1)}, u32[]{:S(2)}, u32[]{:S(2)}) collective-permute-start(bf16[512,512]{1,0:T(8,128)(2,1)} %bitcast.1), channel_id=1, source_target_pairs={{0,16},{16,0},{1,17},{17,1},{2,18},{18,2},{3,19},{19,3},{4,20},{20... | collective-permute-start | bytes 1572872 | tf_op jit(solution)/shard_map/ppermute | solution.py:301
  40.8 78.9 %copy-start.10 = (bf16[1,2560,512]{2,1,0:T(8,128)(2,1)S(1)}, bf16[1,2560,512]{2,1,0:T(8,128)(2,1)}, u32[]{:S(2)}) copy-start(bf16[1,2560,512]{2,1,0:T(8,128)(2,1)} %param.8) | copy-start | bytes 7864324
  122.9 1.3 copy-start.8
  124.2 17.5 %copy-start.4 = (bf16[8,128,512]{2,1,0:T(8,128)(2,1)S(1)}, bf16[8,128,512]{2,1,0:T(8,128)(2,1)}, u32[]{:S(2)}) copy-start(bf16[8,128,512]{2,1,0:T(8,128)(2,1)} %pad_maximum_fusion.1.x_ref) | copy-start | bytes 3145732
  124.3 2.0 collective-permute-start.4
  127.7 14.0 %collective-permute-start.5 = (bf16[512,512]{1,0:T(8,128)(2,1)S(1)}, bf16[512,512]{1,0:T(8,128)(2,1)S(1)}, u32[]{:S(2)}, u32[]{:S(2)}) collective-permute-start(bf16[512,512]{1,0:T(8,128)(2,1)S(1)} %add_convert_fusion.2), channel_id=1, source_target_pairs={{0,1},{1,0},{2,3},{3,2},{4,5},{5,4},{6,7},{7,6},{8,9},{9,8},{10,11... | collective-permute-start | bytes 1572872 | tf_op jit(solution)/shard_map/ppermute | solution.py:347
  141.9 2.0 collective-permute-start.6
  144.0 0.8 copy-start.5
  144.0 1.9 copy-start.6
  222.9 4.4 %copy-start.1 = (bf16[8,128,1280]{2,1,0:T(8,128)(2,1)S(1)}, bf16[8,128,1280]{2,1,0:T(8,128)(2,1)}, u32[]{:S(2)}) copy-start(bf16[8,128,1280]{2,1,0:T(8,128)(2,1)} %layer0.1) | copy-start | bytes 7864324
  222.9 4.4 %copy-start.2 = (bf16[8,128,1280]{2,1,0:T(8,128)(2,1)S(1)}, bf16[8,128,1280]{2,1,0:T(8,128)(2,1)}, u32[]{:S(2)}) copy-start(bf16[8,128,1280]{2,1,0:T(8,128)(2,1)} %layer1.1) | copy-start | bytes 7864324
  227.2 2.7 collective-permute-start.7
  229.4 42.0 %collective-permute-start.10 = (bf16[1024,1280]{1,0:T(8,128)(2,1)}, bf16[1024,1280]{1,0:T(8,128)(2,1)}, u32[]{:S(2)}, u32[]{:S(2)}) collective-permute-start(bf16[1024,1280]{1,0:T(8,128)(2,1)} %broadcast_select_fusion.2), channel_id=1, source_target_pairs={{0,16},{16,0},{1,17},{17,1},{2,18},{18,2},{3,19},{19,3},{4,20},{20... | collective-permute-start | bytes 7864328 | tf_op jit(solution)/shard_map/ppermute | solution.py:301
  230.8 14.2 %collective-permute-start.8 = (bf16[512,512]{1,0:T(8,128)(2,1)}, bf16[512,512]{1,0:T(8,128)(2,1)}, u32[]{:S(2)}, u32[]{:S(2)}) collective-permute-start(bf16[512,512]{1,0:T(8,128)(2,1)} %add_convert_fusion.1), channel_id=1, source_target_pairs={{0,1},{1,0},{2,3},{3,2},{4,5},{5,4},{6,7},{7,6},{8,9},{9,8},{10,11... | collective-permute-start | bytes 1572872 | tf_op jit(solution)/shard_map/ppermute | solution.py:347
  234.6 30.2 %all-to-all-start.2 = ((bf16[128,8,512]{0,2,1:T(8,128)(2,1)}), bf16[128,8,512]{0,2,1:T(8,128)(2,1)}, u32[]{:S(2)}, u32[]{:S(2)}) async-start(bf16[128,8,512]{0,2,1:T(8,128)(2,1)} %bitcast.51), calls=%async_computation.2 | async-start | bytes 2097152 | tf_op jit(solution)/shard_map/all_to_all | solution.py:306
  246.9 2.1 copy-start.3
  246.9 2.0 collective-permute-start.9
  264.8 29.8 %all-to-all-start.1 = ((bf16[8,128,512]{2,1,0:T(8,128)(2,1)}), bf16[8,128,512]{2,1,0:T(8,128)(2,1)}, u32[]{:S(2)}, u32[]{:S(2)}) async-start(bf16[8,128,512]{2,1,0:T(8,128)(2,1)} %broadcast_select_fusion.4), calls=%async_computation.1 | async-start | bytes 2097152 | tf_op jit(solution)/shard_map/all_to_all | solution.py:358
  271.4 3.1 %copy-start.9 = (bf16[8,128,512]{2,1,0:T(8,128)(2,1)S(1)}, bf16[8,128,512]{2,1,0:T(8,128)(2,1)}, u32[]{:S(2)}) copy-start(bf16[8,128,512]{2,1,0:T(8,128)(2,1)} %copy.14) | copy-start | bytes 3145732

commit v3 on v2

--- a/solution.py
+++ b/solution.py
@@ -32,13 +32,18 @@
 
 
 def layer_kernel(
-    dp_count,
+    sizes,
     inner,
     width,
+    layer,
+    is_last,
     x_ref,
     gain_ref,
     up_ref,
+    down_ref,
     hid_out,
+    x_out,
+    state_out,
     scaled,
     sum_send,
     sum_recv,
@@ -48,6 +53,10 @@
     z_recv,
     total,
     hid,
+    part_send,
+    part_recv,
+    x_next,
+    state_buf,
     sum_ss,
     sum_rs,
     x_ss,
@@ -61,8 +70,22 @@
     fx_ss,
     fx_rs,
     out_sem,
+    part_ss,
+    part_rs,
+    xn_ss,
+    xn_rs,
+    st_ss,
+    st_rs,
+    end_sem,
 ):
+    sections, dp_count, tensors = sizes
     outer = dp_count // inner
+    group = sections * tensors
+    owned = dp_count // group
+    per_tensor = dp_count // tensors
+    core = lax.axis_index("section")
+    tensor = lax.axis_index("tensor")
+    member = tensor * sections + core
     me = lax.axis_index("dp")
     z = me // inner
     x = lax.rem(me, inner)
@@ -74,7 +97,32 @@
         pl.semaphore_signal(
             barrier, inc=1, device_id={"dp": lax.rem(me + m, dp_count)}, device_id_type=MESH
         )
-    pl.semaphore_wait(barrier, dp_count - 1)
+
+    def place(index):
+        return {"section": lax.rem(index, sections), "tensor": index // sections}
+
+    for off in range(1, group):
+        pl.semaphore_signal(
+            barrier, inc=1, device_id=place(lax.rem(member + off, group)), device_id_type=MESH
+        )
+    giver = lax.rem(me, group)
+    for q in range(per_tensor):
+        source = tensor * per_tensor + q
+        apart = (giver != member) | (source != me)
+
+        @pl.when((core == layer) & apart)
+        def _():
+            pl.semaphore_signal(
+                barrier, inc=1, device_id={"dp": source, **place(giver)}, device_id_type=MESH
+            )
+
+    def state_is_local(block):
+        return (core == layer) & (block == me) & (tensor == me // per_tensor)
+
+    arrivals = dp_count - 1 + group - 1 + owned
+    for i in range(owned):
+        arrivals = arrivals - state_is_local(member + i * group).astype(jnp.int32)
+    pl.semaphore_wait(barrier, arrivals)
 
     row_id = lax.broadcasted_iota(jnp.int32, (rows, rows), 0)
     col_id = lax.broadcasted_iota(jnp.int32, (rows, rows), 1)
@@ -177,48 +225,192 @@
     def store(block):
         return pltpu.make_async_copy(hid.at[block], hid_out.at[block], out_sem.at[block])
 
+    def part_copy(block):
+        return remote(
+            part_send.at[block],
+            part_recv.at[block // group, member],
+            part_ss.at[block],
+            part_rs.at[(block // group) * group + member],
+            place(lax.rem(block, group)),
+        )
+
+    def part_landing(block, off):
+        source = lax.rem(member + off, group)
+        return remote(
+            part_send.at[block],
+            part_recv.at[block // group, source],
+            part_ss.at[block],
+            part_rs.at[(block // group) * group + source],
+            place(source),
+        )
+
+    def next_copy(block, off):
+        return remote(
+            x_next.at[block],
+            x_next.at[block],
+            xn_ss.at[(block // group) * group + off],
+            xn_rs.at[block],
+            place(lax.rem(member + off, group)),
+        )
+
+    slot = lax.rem(me, per_tensor)
+
+    def state_copy(block):
+        return remote(
+            x_next.at[block],
+            state_buf.at[slot],
+            st_ss.at[block // group],
+            st_rs.at[slot],
+            {"section": layer, "dp": block, "tensor": me // per_tensor},
+        )
+
+    def state_local(block):
+        return pltpu.make_async_copy(x_next.at[block], state_buf.at[slot], st_rs.at[slot])
+
+    def finish(block):
+        @pl.when(lax.rem(block, group) == member)
+        def _():
+            sum_now = part_send[block].astype(F32)
+            for off in range(1, group):
+                part_landing(block, off).wait_recv()
+                sum_now = sum_now + part_recv[
+                    block // group, lax.rem(member + off, group)
+                ].astype(F32)
+            x_next[block] = (x_ref[block].astype(F32) + sum_now).astype(BF16)
+            if not is_last:
+                for off in range(1, group):
+                    next_copy(block, off).start()
+            local = state_is_local(block)
+
+            @pl.when(local)
+            def _():
+                state_local(block).start()
+
+            @pl.when(jnp.logical_not(local))
+            def _():
+                state_copy(block).start()
+
+    waiting = []
+
+    def finish_oldest():
+        valid, block = waiting.pop(0)
+        if valid is None:
+            finish(block)
+        else:
+            pl.when(valid)(lambda: finish(block))
+
+    def use(block):
+        store(block).start()
+        part_send[block] = jnp.dot(
+            hid[block], down_ref[...], preferred_element_type=F32
+        ).astype(BF16)
+
+        @pl.when(lax.rem(block, group) != member)
+        def _():
+            part_copy(block).start()
+
+    def queue(valid, block):
+        waiting.append((valid, block))
+        if len(waiting) > 3:
+            finish_oldest()
+
     last = outer - 1
-    for j in range(outer):
+
+    def start_hops(j):
+        @pl.when((z - j >= 0) & (z < last))
+        def _():
+            hop(z - j, z + 1, up_ss, up_rs, j).start()
+
+        @pl.when((z + j <= last) & (z > 0))
+        def _():
+            hop(z + j, z - 1, dn_ss, dn_rs, j).start()
+
+    def use_peers(j):
+        if j == 0:
+            expect(z, 0).wait_recv()
+            use(z * inner + peer)
+            queue(None, z * inner + peer)
+            return
+        for valid, origin, sem_id in (
+            (z - j >= 0, z - j, j),
+            (z + j <= last, z + j, last + j),
+        ):
+
+            @pl.when(valid)
+            def _():
+                expect(origin, sem_id).wait_recv()
+                use(origin * inner + peer)
+
+            queue(valid, origin * inner + peer)
+
+    start_hops(0)
+    forward(z, 0).start()
+    use(me)
+    queue(None, me)
+    for j in range(1, outer):
+        above, below = z - j >= 0, z + j <= last
+
+        @pl.when(above)
+        def _():
+            landing(z - j, up_ss, up_rs, j - 1).wait_recv()
+            forward(z - j, j).start()
+
+        @pl.when(below)
+        def _():
+            landing(z + j, dn_ss, dn_rs, j - 1).wait_recv()
+            forward(z + j, last + j).start()
+
         if j < last:
-
-            @pl.when((z - j >= 0) & (z < last))
+            start_hops(j)
+        for valid, origin in ((above, z - j), (below, z + j)):
+            pl.when(valid)(lambda: use(origin * inner + x))
+            queue(valid, origin * inner + x)
+        use_peers(j - 1)
+    use_peers(last)
+    while waiting:
+        finish_oldest()
+
+    if not is_last:
+        for block in range(dp_count):
+
+            @pl.when(block % group != member)
             def _():
-                hop(z - j, z + 1, up_ss, up_rs, j).start()
-
-            @pl.when((z + j <= last) & (z > 0))
-            def _():
-                hop(z + j, z - 1, dn_ss, dn_rs, j).start()
-
-        if j == 0:
-            forward(z, 0).start()
-            store(me).start()
-        if j < last:
-
-            @pl.when(z - 1 - j >= 0)
-            def _():
-                landing(z - 1 - j, up_ss, up_rs, j).wait_recv()
-                forward(z - 1 - j, 1 + j).start()
-                store((z - 1 - j) * inner + x).start()
-
-            @pl.when(z + 1 + j <= last)
-            def _():
-                landing(z + 1 + j, dn_ss, dn_rs, j).wait_recv()
-                forward(z + 1 + j, outer + j).start()
-                store((z + 1 + j) * inner + x).start()
-
-    expect(z, 0).wait_recv()
-    store(z * inner + peer).start()
-    for j in range(last):
-
-        @pl.when(z - 1 - j >= 0)
-        def _():
-            expect(z - 1 - j, 1 + j).wait_recv()
-            store((z - 1 - j) * inner + peer).start()
-
-        @pl.when(z + 1 + j <= last)
-        def _():
-            expect(z + 1 + j, outer + j).wait_recv()
-            store((z + 1 + j) * inner + peer).start()
+                next_copy(block, 0).wait_recv()
+
+        pltpu.make_async_copy(x_next, x_out, end_sem.at[0]).start()
+
+    @pl.when(core == layer)
+    def _():
+        stores = []
+        for q in range(per_tensor):
+            pltpu.make_async_copy(x_next.at[0], state_buf.at[q], st_rs.at[q]).wait()
+            copy = pltpu.make_async_copy(
+                state_buf.at[q],
+                state_out.at[:, pl.ds(q * x_ref.shape[2], x_ref.shape[2])],
+                end_sem.at[1 + q],
+            )
+            copy.start()
+            stores.append(copy)
+        for copy in stores:
+            copy.wait()
+
+    if not is_last:
+        pltpu.make_async_copy(x_next, x_out, end_sem.at[0]).wait()
+    for block in range(dp_count):
+
+        @pl.when(block % group != member)
+        def _():
+            part_copy(block).wait_send()
+
+    for i in range(owned):
+        block = member + i * group
+        if not is_last:
+            for off in range(1, group):
+                next_copy(block, off).wait_send()
+
+        @pl.when(jnp.logical_not(state_is_local(block)))
+        def _():
+            state_copy(block).wait_send()
 
     for copy in list(x_copies.values()) + list(z_copies.values()) + sum_copies:
         copy.wait_send()
@@ -245,24 +437,34 @@
         store(block).wait()
 
 
-def layer_hidden(layer, dp_count, width, x, gain_row, up):
-    rows = x.shape[0] // dp_count
-    slice_width = x.shape[1]
+def layer_step(layer, sizes, width, x, gain_row, up, down):
+    sections, dp_count, tensors = sizes
+    rows, slice_width = x.shape[1:]
     half = up.shape[1]
     inner = 2
-    assert dp_count % inner == 0
+    group = sections * tensors
+    assert dp_count % inner == 0 and dp_count % group == 0
     outer = dp_count // inner
+    per_tensor = dp_count // tensors
+    is_last = layer == sections - 1
     dma = pltpu.SemaphoreType.DMA
     vmem = pl.BlockSpec(memory_space=pltpu.VMEM)
+    hbm = pl.BlockSpec(memory_space=pl.ANY)
     wide = pltpu.VMEM((outer, rows, half), BF16)
-    hidden = pl.pallas_call(
-        functools.partial(layer_kernel, dp_count, inner, width),
+    thin = pltpu.VMEM((dp_count, rows, slice_width), BF16)
+    x_shape = x.shape if not is_last else (1, 8, 128)
+    return pl.pallas_call(
+        functools.partial(layer_kernel, sizes, inner, width, layer, is_last),
         name=f"layer{layer}",
-        out_shape=jax.ShapeDtypeStruct((dp_count, rows, half), BF16),
-        in_specs=[vmem] * 3,
-        out_specs=pl.BlockSpec(memory_space=pl.ANY),
+        out_shape=(
+            jax.ShapeDtypeStruct((dp_count, rows, half), BF16),
+            jax.ShapeDtypeStruct(x_shape, BF16),
+            jax.ShapeDtypeStruct((rows, per_tensor * slice_width), BF16),
+        ),
+        in_specs=[vmem] * 4,
+        out_specs=(hbm, hbm, hbm),
         scratch_shapes=[
-            pltpu.VMEM((dp_count, rows, slice_width), BF16),
+            thin,
             pltpu.VMEM((dp_count, 1, rows), F32),
             pltpu.VMEM((dp_count, 1, rows), F32),
             wide,
@@ -271,14 +473,19 @@
             wide,
             pltpu.VMEM((rows, half), F32),
             pltpu.VMEM((dp_count, rows, half), BF16),
+            thin,
+            pltpu.VMEM((dp_count // group, group, rows, slice_width), BF16),
+            thin,
+            pltpu.VMEM((per_tensor, rows, slice_width), BF16),
         ]
         + [dma((dp_count,))] * 2
         + [dma((outer,))] * 8
         + [dma((2 * outer,))] * 2
-        + [dma((dp_count,))],
+        + [dma((dp_count,))]
+        + [dma((dp_count,))] * 4
+        + [dma((dp_count // group,)), dma((per_tensor,)), dma((1 + per_tensor,))],
         compiler_params=pltpu.CompilerParams(collective_id=layer, has_side_effects=True),
-    )(x.reshape(dp_count, rows, slice_width), gain_row, up)
-    return hidden.reshape(dp_count * rows, half)
+    )(x, gain_row, up, down)
 
 
 def body(tokens, gain, w_up, w_down, cotangent):
@@ -287,7 +494,6 @@
     assert layers == 2
     dp_id = lax.axis_index("dp")
     dp_count = lax.axis_size("dp")
-    tensor_id = lax.axis_index("tensor")
     tensor_count = lax.axis_size("tensor")
     rows, own_width = tokens.shape
     width = own_width * tensor_count
@@ -333,30 +539,15 @@
 
     states = []
     hiddens = []
+    sizes = (layers, dp_count, tensor_count)
+    x = x.reshape(dp_count, rows, slice_width)
     for layer in range(layers):
-        x_f = x.astype(F32)
-        hidden_all = layer_hidden(layer, dp_count, width, x, gains[layer], up_parts[layer])
-        hiddens.append(hidden_all)
-        out = jnp.dot(hidden_all, down_parts[layer], preferred_element_type=F32)
-        mid = all_rows // layers
-        keep = lax.dynamic_slice_in_dim(out, core * mid, mid, 0)
-        give = lax.dynamic_slice_in_dim(out, other * mid, mid, 0).astype(BF16)
-        summed = keep + swap(give).astype(F32)
-        if tensor_count == 2:
-            sent = summed.astype(BF16)
-            got = lax.ppermute(sent, "tensor", [(0, 1), (1, 0)])
-            summed = sent.astype(F32) + got.astype(F32)
-        else:
-            summed = lax.psum(summed.astype(BF16), "tensor").astype(F32)
-        x_mid = lax.dynamic_slice_in_dim(x_f, core * mid, mid, 0)
-        new_mid = (x_mid + summed).astype(BF16)
-        new_a, new_b = both(new_mid, swap(new_mid))
-        x = jnp.concatenate([new_a, new_b], axis=0)
-        states.append(x)
-
-    state_own = jnp.where(core == 0, states[0], states[1])
-    state_rows = lax.all_to_all(state_own, "dp", split_axis=0, concat_axis=1, tiled=True)
-    state = lax.dynamic_slice_in_dim(state_rows, tensor_id * own_width, own_width, 1)
+        hidden, x, state = layer_step(
+            layer, sizes, width, x, gains[layer], up_parts[layer], down_parts[layer]
+        )
+        hiddens.append(hidden.reshape(all_rows, half))
+        states.append(state)
+    state = jnp.where(core == 0, states[0], states[1])
 
     hid_keep = jnp.where(core == 0, hiddens[0], hiddens[1])
     hid_got = swap(jnp.where(core == 0, hiddens[1], hiddens[0]))

time: 298 us -> 278 us (0.933)
  waiting for transfers between devices: 61.6 us -> 31.1 us
  Pallas kernels: 156 us -> 178 us
  matrix products: 11.8 us -> 4.28 us
  local copies, waits for them, and re-layouts: 15.4 us -> 10.4 us
    pallas_call x2, Pallas kernels: 156 us -> 178 us  [layer_step(): pl.pallas_call(functools.partial(layer_kernel, sizes, inner, width, layer...]
    ppermute x2 -> x0, waiting for transfers between devices: 18.4 us -> none  [body(): got = lax.ppermute(sent, 'tensor', [(0, 1), (1, 0)])]
    all_to_all x1 -> x0, waiting for transfers between devices: 15.9 us -> none  [body(): lax.all_to_all(state_own, 'dp', split_axis=0, concat_axis=1, tiled=True)]
    all_to_all x1, waiting for transfers between devices: 14.7 us -> 24.1 us  [body(): lax.all_to_all(cotangent[0], 'dp', split_axis=1, concat_axis=0, tiled=True)]
    all_to_all x1, starting transfers between devices: 4.42 us -> 13 us  [body(): lax.all_to_all(cotangent[0], 'dp', split_axis=1, concat_axis=0, tiled=True)]
    dot_general x2 -> x0, matrix products: 7.49 us -> none  [body(): out = jnp.dot(hidden_all, down_parts[layer], preferred_element_type=F32)]
    ppermute x9 -> x5, waiting for transfers between devices: 6.84 us -> 1.16 us  [swap(): return lax.ppermute(array, 'section', [(0, 1), (1, 0)])]
    convert_element_type x4 -> x0, other arithmetic: 4.4 us -> none  [the longest x2 2.35 us: body(): sent = summed.astype(BF16)]
  transfers between devices with their start and end apart: 14 -> 7, of which waited for: 9 -> 3; matrix products, arithmetic and copies ran while one was open for 9% -> 6% of each run, Pallas kernels for 27% -> 0%
where the time goes in v3:
time: 278 us; the launch traced here: 277 us
  Pallas kernels  178 us (64%)
  waiting for transfers between devices  31.1 us (11%)
  starting transfers between devices  19.6 us (7%)
  other arithmetic  18.1 us (7%)
  blocking collectives  14.6 us (5%)
  local copies, waits for them, and re-layouts  10.4 us (4%)
  matrix products  4.28 us (2%)
    pallas_call x2, Pallas kernels, layer_step(): pl.pallas_call(functools.partial(layer_kernel, sizes, inner, width, layer...  178 us
    all_to_all x1, waiting for transfers between devices, body(): lax.all_to_all(cotangent[0], 'dp', split_axis=1, concat_axis=0, tiled=True)  24.1 us
    all_to_all x1, starting transfers between devices, body(): lax.all_to_all(cotangent[0], 'dp', split_axis=1, concat_axis=0, tiled=True)  13 us
    select_n x5, other arithmetic, both(): return (jnp.where(core == 0, own, got), jnp.where(core == 0, got, own))  10.7 us
    all_gather x1, blocking collectives, body(): tok_full = lax.all_gather(tok_half, 'tensor', axis=1, tiled=True)  10.3 us
    all_to_all x1, starting transfers between devices, body(): lax.all_to_all(tok_full, 'dp', split_axis=1, concat_axis=0, tiled=True)  6.02 us
    all_to_all x1, waiting for transfers between devices, body(): lax.all_to_all(tok_full, 'dp', split_axis=1, concat_axis=0, tiled=True)  5.78 us
  transfers between devices with their start and end apart: 7, of which 3 were waited for; matrix products, arithmetic and copies ran while one was open for 6% of the time, Pallas kernels for 0%

profile of v3, /device:TPU:0, one launch (start us, length us, event | category | flops | bytes accessed | tf_op | source)
XLA Modules:
  0.0 277.1 jit_solution(5541077793223817946)
XLA Ops:
  0.6 0.0 copy-start
  0.7 2.5 dynamic-slice_bitcast_fusion
  3.2 0.5 collective-permute-start.3
  3.7 0.0 copy-start.4
  3.7 0.0 copy-start.1
  3.7 10.3 %all_gather.6 = bf16[64,4096]{1,0:T(8,128)(2,1)S(1)} all-gather(bf16[64,2048]{1,0:T(8,128)(2,1)S(1)} %constant_dynamic-slice_fusion.1), channel_id=1, replica_groups=mesh['section'=2,'dp'=8,'tensor'=2] {'tensor'}, dimensions={1}, use_global_device_ids=true | all-gather | bytes 786432 | tf_op jit(solution)/shard_map/all_gather | solution.py:516
  14.0 0.8 copy.19
  14.8 6.0 %all-to-all-start = ((bf16[64,8,512]{2,0,1:T(8,128)(2,1)}), bf16[64,8,512]{2,0,1:T(8,128)(2,1)}, u32[]{:S(2)}, u32[]{:S(2)}) async-start(bf16[64,8,512]{2,0,1:T(8,128)(2,1)} %bitcast.34), calls=%async_computation | async-start | bytes 1048576 | tf_op jit(solution)/shard_map/all_to_all | solution.py:517
  20.9 2.5 dynamic-slice_bitcast_fusion.1
  23.3 0.0 collective-permute-start.2
  23.3 4.3 %all_gather.7 = bf16[1,4096]{1,0:T(2,128)(2,1)S(1)} all-gather(bf16[1,2048]{1,0:T(2,128)(2,1)S(1)} %copy-done.4), channel_id=1, replica_groups=mesh['section'=2,'dp'=8,'tensor'=2] {'tensor'}, dimensions={1}, use_global_device_ids=true | all-gather | bytes 12288 | tf_op jit(solution)/shard_map/all_gather | solution.py:527
  27.7 0.0 collective-permute-start.1
  27.7 1.1 collective-permute-done.1
  28.9 0.6 broadcast_select_fusion.4
  29.5 5.8 %all-to-all-done = bf16[64,8,512]{2,0,1:T(8,128)(2,1)} async-done(((bf16[64,8,512]{2,0,1:T(8,128)(2,1)}), bf16[64,8,512]{2,0,1:T(8,128)(2,1)}, u32[]{:S(2)}, u32[]{:S(2)}) %all-to-all-start) | async-done | bytes 524320 | tf_op jit(solution)/shard_map/all_to_all | solution.py:517
  35.3 0.0 collective-permute-start
  35.3 0.0 collective-permute-done.3
  35.3 3.5 %bitcast_select_fusion.2 = (bf16[1280,512]{1,0:T(8,128)(2,1)}, bf16[1280,512]{1,0:T(8,128)(2,1)}) fusion(bf16[1280,512]{1,0:T(8,128)(2,1)} %collective-permute-done.3, pred[]{:T(512)S(6)} %eq.2, bf16[1,2560,512]{2,1,0:T(8,128)(2,1)S(1)} %copy-done.1, s32[]{:T(128)S(6)} %select_n.107), kind=kLoop, calls=%fused_computation.10 | loop fusion | flops 1310720 | bytes 5242885 | tf_op jit(solution)/shard_map/jit(_where)/select_n | solution.py:510
  38.7 0.0 collective-permute-done.2
  38.7 3.3 %bitcast_select_fusion.4 = (bf16[512,1280]{1,0:T(8,128)(2,1)}, bf16[512,1280]{1,0:T(8,128)(2,1)}) fusion(bf16[512,1280]{1,0:T(8,128)(2,1)} %collective-permute-done.2, pred[]{:T(512)S(6)} %eq.2, bf16[1,512,2560]{2,1,0:T(8,128)(2,1)S(1)} %copy-done.2, s32[]{:T(128)S(6)} %select_n.107), kind=kLoop, calls=%fused_computation.12 | loop fusion | flops 1310720 | bytes 5242885 | tf_op jit(solution)/shard_map/jit(_where)/select_n | solution.py:510
  42.1 1.2 broadcast_select_fusion.3
  43.2 1.1 pad_maximum_fusion.x_ref
  44.4 95.2 %layer0.1 = (bf16[8,128,1280]{2,1,0:T(8,128)(2,1)}, bf16[8,128,512]{2,1,0:T(8,128)(2,1)}, bf16[128,2048]{1,0:T(8,128)(2,1)}) custom-call(bf16[8,128,512]{2,1,0:T(8,128)(2,1)} %pad_maximum_fusion.x_ref, bf16[1,512]{1,0:T(2,128)(2,1)} %get-tuple-element.23.gain_ref, bf16[512,1280]{1,0:T(8,128)(2,1)} %get-tuple-element.19.up_ref, ...), custom_call_target="tpu_custom_call" | custom-call | tf_op jit(solution)/shard_map/layer0/pallas_call | solution.py:456
  139.6 83.1 %layer1.1 = (bf16[8,128,1280]{2,1,0:T(8,128)(2,1)}, bf16[1,8,128]{2,1,0:T(8,128)(2,1)}, bf16[128,2048]{1,0:T(8,128)(2,1)}) custom-call(bf16[8,128,512]{2,1,0:T(8,128)(2,1)} %get-tuple-element.8.x_ref, bf16[1,512]{1,0:T(2,128)(2,1)} %get-tuple-element.22.gain_ref, bf16[512,1280]{1,0:T(8,128)(2,1)} %get-tuple-element.18.up_ref, ...), custom_call_target="tpu_custom_call" | custom-call | tf_op jit(solution)/shard_map/layer1/pallas_call | solution.py:456
  222.7 4.4 %broadcast_select_fusion.1 = (bf16[8,128,1280]{2,1,0:T(8,128)(2,1)S(1)}, bf16[8,128,1280]{2,1,0:T(8,128)(2,1)}) fusion(bf16[8,128,1280]{2,1,0:T(8,128)(2,1)} %get-tuple-element.10, bf16[8,128,1280]{2,1,0:T(8,128)(2,1)} %get-tuple-element.11, pred[]{:T(512)S(6)} %eq.2), kind=kLoop, calls=%fused_computation.9 | loop fusion | flops 2621440 | bytes 10485761 | tf_op jit(solution)/shard_map/jit(_where)/select_n | solution.py:552
  227.1 2.3 copy.15
  229.3 13.0 %all-to-all-start.1 = ((bf16[128,8,512]{0,2,1:T(8,128)(2,1)}), bf16[128,8,512]{0,2,1:T(8,128)(2,1)}, u32[]{:S(2)}, u32[]{:S(2)}) async-start(bf16[128,8,512]{0,2,1:T(8,128)(2,1)} %bitcast.33), calls=%async_computation.1 | async-start | bytes 2097152 | tf_op jit(solution)/shard_map/all_to_all | solution.py:512
  242.4 1.9 select_bitcast_fusion
  244.3 24.1 %all-to-all-done.1 = bf16[128,8,512]{0,2,1:T(8,128)(2,1)} async-done(((bf16[128,8,512]{0,2,1:T(8,128)(2,1)}), bf16[128,8,512]{0,2,1:T(8,128)(2,1)}, u32[]{:S(2)}, u32[]{:S(2)}) %all-to-all-start.1) | async-done | bytes 1048608 | tf_op jit(solution)/shard_map/all_to_all | solution.py:512
  268.4 2.3 copy.16
  270.7 2.2 bitcast_select_fusion.1
  272.9 4.3 %fusion.7 = bf16[1,2560,512]{2,1,0:T(8,128)(2,1)} fusion(bf16[1024,512]{1,0:T(8,128)(2,1)S(1)} %bitcast.38, bf16[1024,1280]{1,0:T(8,128)(2,1)S(1)} %get-tuple-element.13, bf16[1024,1280]{1,0:T(8,128)(2,1)S(1)} %get-tuple-element.12), kind=kOutput, calls=%fused_computation.5 | convolution fusion | flops 2696151040 | bytes 8912896 | tf_op jit(solution)/shard_map/dot_general | solution.py:556
  (12 shorter events, 0.0 us)
Async XLA Ops:
  0.6 3.0 %copy-start = (bf16[128,2048]{1,0:T(8,128)(2,1)S(1)}, bf16[128,2048]{1,0:T(8,128)(2,1)}, u32[]{:S(2)}) copy-start(bf16[128,2048]{1,0:T(8,128)(2,1)} %param.5) | copy-start | bytes 1572868
  3.2 32.1 %collective-permute-start.3 = (bf16[1280,512]{1,0:T(8,128)(2,1)}, bf16[1280,512]{1,0:T(8,128)(2,1)}, u32[]{:S(2)}, u32[]{:S(2)}) collective-permute-start(bf16[1280,512]{1,0:T(8,128)(2,1)} %dynamic-slice_bitcast_fusion), channel_id=1, source_target_pairs={{0,16},{16,0},{1,17},{17,1},{2,18},{18,2},{3,19},{19,3},{4,20},{20... | collective-permute-start | bytes 3932168 | tf_op jit(solution)/shard_map/ppermute | solution.py:507
  3.7 19.6 %copy-start.4 = (bf16[1,2048]{1,0:T(2,128)(2,1)S(1)}, bf16[1,2048]{1,0:T(2,128)(2,1)}, u32[]{:S(2)}) copy-start(bf16[1,2048]{1,0:T(2,128)(2,1)} %param.6) | copy-start | bytes 12292
  3.7 31.6 %copy-start.1 = (bf16[1,2560,512]{2,1,0:T(8,128)(2,1)S(1)}, bf16[1,2560,512]{2,1,0:T(8,128)(2,1)}, u32[]{:S(2)}) copy-start(bf16[1,2560,512]{2,1,0:T(8,128)(2,1)} %param.8) | copy-start | bytes 7864324
  14.8 20.4 %all-to-all-start = ((bf16[64,8,512]{2,0,1:T(8,128)(2,1)}), bf16[64,8,512]{2,0,1:T(8,128)(2,1)}, u32[]{:S(2)}, u32[]{:S(2)}) async-start(bf16[64,8,512]{2,0,1:T(8,128)(2,1)} %bitcast.34), calls=%async_computation | async-start | bytes 1048576 | tf_op jit(solution)/shard_map/all_to_all | solution.py:517
  23.3 15.4 %collective-permute-start.2 = (bf16[512,1280]{1,0:T(8,128)(2,1)}, bf16[512,1280]{1,0:T(8,128)(2,1)}, u32[]{:S(2)}, u32[]{:S(2)}) collective-permute-start(bf16[512,1280]{1,0:T(8,128)(2,1)} %dynamic-slice_bitcast_fusion.1), channel_id=1, source_target_pairs={{0,16},{16,0},{1,17},{17,1},{2,18},{18,2},{3,19},{19,3},{4,20},{20... | collective-permute-start | bytes 3932168 | tf_op jit(solution)/shard_map/ppermute | solution.py:507
  27.7 1.2 collective-permute-start.1
  35.3 3.5 %copy-start.2 = (bf16[1,512,2560]{2,1,0:T(8,128)(2,1)S(1)}, bf16[1,512,2560]{2,1,0:T(8,128)(2,1)}, u32[]{:S(2)}) copy-start(bf16[1,512,2560]{2,1,0:T(8,128)(2,1)} %param.7) | copy-start | bytes 7864324
  35.3 6.8 %collective-permute-start = (bf16[512,512]{1,0:T(8,128)(2,1)}, bf16[512,512]{1,0:T(8,128)(2,1)S(1)}, u32[]{:S(2)}, u32[]{:S(2)}) collective-permute-start(bf16[512,512]{1,0:T(8,128)(2,1)} %bitcast.1), channel_id=1, source_target_pairs={{0,16},{16,0},{1,17},{17,1},{2,18},{18,2},{3,19},{19,3},{4,20},{20... | collective-permute-start | bytes 1572872 | tf_op jit(solution)/shard_map/ppermute | solution.py:507
  227.1 43.6 %collective-permute-start.4 = (bf16[1024,1280]{1,0:T(8,128)(2,1)}, bf16[1024,1280]{1,0:T(8,128)(2,1)}, u32[]{:S(2)}, u32[]{:S(2)}) collective-permute-start(bf16[1024,1280]{1,0:T(8,128)(2,1)} %bitcast.11), channel_id=1, source_target_pairs={{0,16},{16,0},{1,17},{17,1},{2,18},{18,2},{3,19},{19,3},{4,20},{20... | collective-permute-start | bytes 7864328 | tf_op jit(solution)/shard_map/ppermute | solution.py:507
  229.3 39.1 %all-to-all-start.1 = ((bf16[128,8,512]{0,2,1:T(8,128)(2,1)}), bf16[128,8,512]{0,2,1:T(8,128)(2,1)}, u32[]{:S(2)}, u32[]{:S(2)}) async-start(bf16[128,8,512]{0,2,1:T(8,128)(2,1)} %bitcast.33), calls=%async_computation.1 | async-start | bytes 2097152 | tf_op jit(solution)/shard_map/all_to_all | solution.py:512
  270.7 2.2 copy-start.3

commit v4 on v3

--- a/solution.py
+++ b/solution.py
@@ -488,20 +488,339 @@
     )(x, gain_row, up, down)
 
 
+def front_kernel(
+    sizes,
+    tok_ref,
+    gain_ref,
+    up_ref,
+    down_ref,
+    cot_ref,
+    x_out,
+    gain_out0,
+    gain_out1,
+    up_out0,
+    up_out1,
+    down_out0,
+    down_out1,
+    cot_out,
+    x_buf,
+    gain_buf,
+    up_buf,
+    down_buf,
+    cot_buf,
+    tok_ss,
+    tok_rs,
+    tf_ss,
+    tf_rs,
+    cot_ss,
+    cot_rs,
+    cy_ss,
+    cy_rs,
+    gain_ss,
+    gain_rs,
+    w_ss,
+    w_rs,
+    own_sem,
+    end_sem,
+):
+    sections, dp_count, tensors = sizes
+    group = sections * tensors
+    per_tensor = dp_count // tensors
+    core = lax.axis_index("section")
+    tensor = lax.axis_index("tensor")
+    me = lax.axis_index("dp")
+    other = 1 - core
+    member = tensor * sections + core
+    rows, slice_width = x_buf.shape[1:]
+    half = up_buf.shape[2]
+    half_rows = rows // sections
+    part_rows = rows // tensors
+
+    def place(index):
+        return {"section": lax.rem(index, sections), "tensor": index // sections}
+
+    barrier = pltpu.get_barrier_semaphore()
+
+    def greet(target):
+        pl.semaphore_signal(barrier, inc=1, device_id=target, device_id_type=MESH)
+
+    for m in range(1, dp_count):
+        greet({"dp": lax.rem(me + m, dp_count)})
+    for off in range(1, group):
+        greet(place(lax.rem(member + off, group)))
+    feature_home = me // per_tensor
+    at_home = feature_home == tensor
+    for source in range(dp_count):
+
+        @pl.when(jnp.logical_not(at_home & (me == source)))
+        def _():
+            greet({"dp": source, "tensor": feature_home})
+
+    self_send = at_home.astype(jnp.int32)
+    pl.semaphore_wait(barrier, dp_count - 1 + group - 1 + per_tensor * tensors - self_send)
+
+    my_half = pl.ds(pl.multiple_of(core * half_rows, half_rows), half_rows)
+    my_part = pl.ds(pl.multiple_of(tensor * part_rows, part_rows), part_rows)
+
+    def columns(index, size):
+        return pl.ds(pl.multiple_of(index * size, size), size)
+
+    def token_copy(q, tt):
+        return remote(
+            tok_ref.at[my_half, pl.ds(q * slice_width, slice_width)],
+            x_buf.at[me, my_half],
+            tok_ss.at[q * tensors + tt],
+            tok_rs.at[me],
+            {"dp": tensor * per_tensor + q, "tensor": tt},
+        )
+
+    def token_local(q):
+        return pltpu.make_async_copy(
+            tok_ref.at[my_half, pl.ds(q * slice_width, slice_width)],
+            x_buf.at[me, my_half],
+            tok_rs.at[me],
+        )
+
+    def is_self(q, tt):
+        return (tensor * per_tensor + q == me) & (tensor == tt)
+
+    for q in range(per_tensor):
+        for tt in range(tensors):
+            local = is_self(q, tt)
+
+            @pl.when(local)
+            def _():
+                token_local(q).start()
+
+            @pl.when(jnp.logical_not(local))
+            def _():
+                token_copy(q, tt).start()
+
+    def gain_copy(off):
+        return remote(
+            gain_ref.at[:, columns(lax.rem(me, per_tensor), slice_width)],
+            gain_buf.at[core],
+            gain_ss.at[off],
+            gain_rs.at[core],
+            place(lax.rem(member + off, group)),
+        )
+
+    gain_local = pltpu.make_async_copy(
+        gain_ref.at[:, columns(lax.rem(me, per_tensor), slice_width)],
+        gain_buf.at[core],
+        gain_rs.at[core],
+    )
+
+    @pl.when(at_home)
+    def _():
+        gain_local.start()
+        for off in range(1, group):
+            gain_copy(off).start()
+
+    def up_half(index):
+        if up_ref.shape[0] == sections:
+            return up_ref.at[index]
+        return up_ref.at[0, :, columns(index, half)]
+
+    give_up = remote(
+        up_half(other),
+        up_buf.at[core],
+        w_ss.at[0],
+        w_rs.at[0],
+        {"section": other},
+    )
+    give_up.start()
+    own_up = pltpu.make_async_copy(
+        up_half(core), up_buf.at[core], own_sem.at[0]
+    )
+    own_up.start()
+
+    cot_copies = []
+    for m in range(1, dp_count):
+        target = lax.rem(me + m, dp_count)
+        copy = remote(
+            cot_ref.at[0, my_part, columns(target, slice_width)],
+            cot_buf.at[me, my_part],
+            cot_ss.at[m],
+            cot_rs.at[m],
+            {"dp": target},
+        )
+        copy.start()
+        cot_copies.append(copy)
+    cot_local = pltpu.make_async_copy(
+        cot_ref.at[0, my_part, columns(me, slice_width)], cot_buf.at[me, my_part], own_sem.at[2]
+    )
+    cot_local.start()
+
+    give_down = remote(
+        down_ref.at[0, columns(other, half), :],
+        down_buf.at[core],
+        w_ss.at[1],
+        w_rs.at[1],
+        {"section": other},
+    )
+    give_down.start()
+    own_down = pltpu.make_async_copy(
+        down_ref.at[0, columns(core, half), :], down_buf.at[core], own_sem.at[1]
+    )
+    own_down.start()
+
+    def token_forward(source):
+        return remote(
+            x_buf.at[source, my_half],
+            x_buf.at[source, my_half],
+            tf_ss.at[source],
+            tf_rs.at[source],
+            {"section": other},
+        )
+
+    their_half = columns(other, half_rows)
+    for source in range(dp_count):
+        pltpu.make_async_copy(
+            x_buf.at[source, my_half], x_buf.at[source, my_half], tok_rs.at[source]
+        ).wait()
+        token_forward(source).start()
+
+    ends = []
+
+    def put(src, dst):
+        copy = pltpu.make_async_copy(src, dst, end_sem.at[len(ends)])
+        copy.start()
+        ends.append(copy)
+
+    own_up.wait()
+    give_up.wait_recv()
+    put(up_buf.at[0], up_out0)
+    put(up_buf.at[1], up_out1)
+    own_down.wait()
+    give_down.wait_recv()
+    put(down_buf.at[0], down_out0)
+    put(down_buf.at[1], down_out1)
+    for layer in range(sections):
+        pltpu.make_async_copy(
+            gain_buf.at[layer], gain_buf.at[layer], gain_rs.at[layer]
+        ).wait()
+    put(gain_buf.at[0], gain_out0)
+    put(gain_buf.at[1], gain_out1)
+
+    def cot_share(m, off):
+        source = lax.rem(me + dp_count - m, dp_count)
+        return remote(
+            cot_buf.at[source, my_part],
+            cot_buf.at[source, my_part],
+            cy_ss.at[m * tensors + off],
+            cy_rs.at[m * tensors + off],
+            {"tensor": lax.rem(tensor + off, tensors)},
+        )
+
+    for m in range(dp_count):
+        if m == 0:
+            cot_local.wait()
+        else:
+            cot_copies[m - 1].wait_recv()
+        for off in range(1, tensors):
+            cot_share(m, off).start()
+
+    for source in range(dp_count):
+        token_forward(source).wait_recv()
+    put(x_buf, x_out)
+    for m in range(dp_count):
+        for off in range(1, tensors):
+            cot_share(m, off).wait_recv()
+    put(cot_buf, cot_out)
+
+    for q in range(per_tensor):
+        for tt in range(tensors):
+
+            @pl.when(jnp.logical_not(is_self(q, tt)))
+            def _():
+                token_copy(q, tt).wait_send()
+
+    @pl.when(at_home)
+    def _():
+        for off in range(1, group):
+            gain_copy(off).wait_send()
+
+    give_up.wait_send()
+    give_down.wait_send()
+    for copy in cot_copies:
+        copy.wait_send()
+    for source in range(dp_count):
+        token_forward(source).wait_send()
+    for m in range(dp_count):
+        for off in range(1, tensors):
+            cot_share(m, off).wait_send()
+    for copy in ends:
+        copy.wait()
+
+
+def front(sizes, tokens, gain, w_up, w_down, cotangent):
+    sections, dp_count, tensors = sizes
+    assert sections == 2
+    group = sections * tensors
+    per_tensor = dp_count // tensors
+    rows, own_width = tokens.shape
+    slice_width = own_width // per_tensor
+    depth = w_up.shape[1]
+    half = w_up.shape[2] // sections
+    dma = pltpu.SemaphoreType.DMA
+    hbm = pl.BlockSpec(memory_space=pl.ANY)
+    if half % 128:
+        w_up = w_up[0].reshape(depth, sections, half).transpose(1, 0, 2)
+
+    def shape(*dims, dtype=BF16):
+        return jax.ShapeDtypeStruct(dims, dtype)
+
+    return pl.pallas_call(
+        functools.partial(front_kernel, sizes),
+        name="front",
+        out_shape=(
+            shape(dp_count, rows, slice_width),
+            shape(1, slice_width, dtype=F32),
+            shape(1, slice_width, dtype=F32),
+            shape(depth, half),
+            shape(depth, half),
+            shape(half, slice_width),
+            shape(half, slice_width),
+            shape(dp_count, rows, slice_width),
+        ),
+        in_specs=[hbm] * 5,
+        out_specs=(hbm,) * 8,
+        scratch_shapes=[
+            pltpu.VMEM((dp_count, rows, slice_width), BF16),
+            pltpu.VMEM((sections, 1, slice_width), F32),
+            pltpu.VMEM((sections, depth, half), BF16),
+            pltpu.VMEM((sections, half, slice_width), BF16),
+            pltpu.VMEM((dp_count, rows, slice_width), BF16),
+            dma((dp_count,)),
+            dma((dp_count,)),
+            dma((dp_count,)),
+            dma((dp_count,)),
+            dma((dp_count,)),
+            dma((dp_count,)),
+            dma((dp_count * tensors,)),
+            dma((dp_count * tensors,)),
+            dma((group,)),
+            dma((sections,)),
+            dma((2,)),
+            dma((2,)),
+            dma((3,)),
+            dma((8,)),
+        ],
+        compiler_params=pltpu.CompilerParams(collective_id=sections, has_side_effects=True),
+    )(tokens, gain.astype(F32), w_up, w_down, cotangent)
+
+
 def body(tokens, gain, w_up, w_down, cotangent):
     core = lax.axis_index("section")
     layers = lax.axis_size("section")
-    assert layers == 2
-    dp_id = lax.axis_index("dp")
     dp_count = lax.axis_size("dp")
     tensor_count = lax.axis_size("tensor")
     rows, own_width = tokens.shape
     width = own_width * tensor_count
-    slice_width = width // dp_count
-    hidden_width = w_up.shape[2]
-    half = hidden_width // layers
-    other = 1 - core
+    half = w_up.shape[2] // layers
     all_rows = rows * dp_count
+    sizes = (layers, dp_count, tensor_count)
 
     def swap(array):
         return lax.ppermute(array, "section", [(0, 1), (1, 0)])
@@ -509,38 +828,12 @@
     def both(own, got):
         return (jnp.where(core == 0, own, got), jnp.where(core == 0, got, own))
 
-    cot_mine = lax.all_to_all(cotangent[0], "dp", split_axis=1, concat_axis=0, tiled=True)
-
-    half_rows = rows // layers
-    tok_half = lax.dynamic_slice_in_dim(tokens, core * half_rows, half_rows, 0)
-    tok_full = lax.all_gather(tok_half, "tensor", axis=1, tiled=True)
-    x_half = lax.all_to_all(tok_full, "dp", split_axis=1, concat_axis=0, tiled=True)
-    x_a, x_b = both(x_half, swap(x_half))
-    x = jnp.concatenate(
-        [
-            x_a.reshape(dp_count, half_rows, slice_width),
-            x_b.reshape(dp_count, half_rows, slice_width),
-        ],
-        axis=1,
-    ).reshape(all_rows, slice_width)
-
-    gain_all = lax.all_gather(gain, "tensor", axis=1, tiled=True)
-    gain_own = lax.dynamic_slice_in_dim(gain_all, dp_id * slice_width, slice_width, 1)
-    gains = both(gain_own, swap(gain_own))
-
-    up_parts = both(
-        lax.dynamic_slice_in_dim(w_up[0], core * half, half, 1),
-        swap(lax.dynamic_slice_in_dim(w_up[0], other * half, half, 1)),
-    )
-    down_parts = both(
-        lax.dynamic_slice_in_dim(w_down[0], core * half, half, 0),
-        swap(lax.dynamic_slice_in_dim(w_down[0], other * half, half, 0)),
-    )
+    x, *rest = front(sizes, tokens, gain, w_up, w_down, cotangent)
+    gains, up_parts, down_parts = rest[0:2], rest[2:4], rest[4:6]
+    cot_mine = rest[6].reshape(all_rows, -1)
 
     states = []
     hiddens = []
-    sizes = (layers, dp_count, tensor_count)
-    x = x.reshape(dp_count, rows, slice_width)
     for layer in range(layers):
         hidden, x, state = layer_step(
             layer, sizes, width, x, gains[layer], up_parts[layer], down_parts[layer]

time: 278 us -> 249 us (0.90); the launches traced: 277 us -> 245 us
  Pallas kernels: 178 us -> 230 us
  waiting for transfers between devices: 31.1 us -> 4.02 us
  starting transfers between devices: 19.6 us -> 0.07 us
  blocking collectives: 14.6 us -> 0 us
  other arithmetic: 18.1 us -> 4.83 us
  local copies, waits for them, and re-layouts: 10.4 us -> 0.72 us
    pallas_call x0 -> x1, Pallas kernels: none -> 45.1 us  [front(): pl.pallas_call(functools.partial(front_kernel, sizes), name='front', out_...]
    all_to_all x2 -> x0, waiting for transfers between devices: 29.9 us -> none  [the longest x1 24.1 us: body(): lax.all_to_all(cotangent[0], 'dp', split_axis=1, concat_axis=0, tiled=True)]
    all_to_all x2 -> x0, starting transfers between devices: 19 us -> none  [the longest x1 13 us: body(): lax.all_to_all(cotangent[0], 'dp', split_axis=1, concat_axis=0, tiled=True)]
    all_gather x2 -> x0, blocking collectives: 14.6 us -> none  [the longest x1 10.3 us: body(): tok_full = lax.all_gather(tok_half, 'tensor', axis=1, tiled=True)]
    select_n x5 -> x1, other arithmetic: 10.7 us -> 0.51 us  [both(): return (jnp.where(core == 0, own, got), jnp.where(core == 0, got, own))]
    pallas_call x2, Pallas kernels: 178 us -> 185 us  [layer_step(): pl.pallas_call(functools.partial(layer_kernel, sizes, inner, width, layer...]
    dynamic_slice x4 -> x0, local copies, waits for them, and re-layouts: 4.99 us -> none  [the longest x1 2.52 us: body(): lax.dynamic_slice_in_dim(w_down[0], other * half, half, 0)]
    all_to_all x2 -> x0, local copies, waits for them, and re-layouts: 3.1 us -> none  [the longest x1 2.27 us: body(): lax.all_to_all(cotangent[0], 'dp', split_axis=1, concat_axis=0, tiled=True)]
  transfers between devices with their start and end apart: 7 -> 1, of which waited for: 3 -> 1; matrix products, arithmetic and copies ran while one was open for 6% -> 0% of each run, Pallas kernels for 0% -> 0%
where the time goes in v4:
time: 249 us; the launch traced here: 245 us
  Pallas kernels  230 us (92%)
  other arithmetic  4.83 us (2%)
  matrix products  4.24 us (2%)
  waiting for transfers between devices  4.02 us (2%)
    pallas_call x2, Pallas kernels, layer_step(): pl.pallas_call(functools.partial(layer_kernel, sizes, inner, width, layer...  185 us
    pallas_call x1, Pallas kernels, front(): pl.pallas_call(functools.partial(front_kernel, sizes), name='front', out_...  45.1 us
  transfers between devices with their start and end apart: 1, of which 1 were waited for; matrix products, arithmetic and copies ran while one was open for 0% of the time, Pallas kernels for 0%

profile of v4, /device:TPU:0, one launch (start us, length us, event | category | flops | bytes accessed | tf_op | source)
XLA Modules:
  0.0 244.9 jit_solution(5202758017311855131)
XLA Ops:
  0.6 1.3 convert_element_type.6.gain_ref
  1.9 45.1 %front.1 = (bf16[8,128,512]{2,1,0:T(8,128)(2,1)}, f32[1,512]{1,0:T(1,128)}, f32[1,512]{1,0:T(1,128)}, bf16[512,1280]{1,0:T(8,128)(2,1)}, bf16[512,1280]{1,0:T(8,...) custom-call(bf16[128,2048]{1,0:T(8,128)(2,1)} %tok_ref.1, ...), custom_call_target="tpu_custom_call" | custom-call | tf_op jit(solution)/shard_map/front/pallas_call | solution.py:774
  47.1 95.3 %layer0.1 = (bf16[8,128,1280]{2,1,0:T(8,128)(2,1)}, bf16[8,128,512]{2,1,0:T(8,128)(2,1)}, bf16[128,2048]{1,0:T(8,128)(2,1)}) custom-call(bf16[8,128,512]{2,1,0:T(8,128)(2,1)} %get-tuple-element.15.x_ref, f32[1,512]{1,0:T(1,128)} %get-tuple-element.16.gain_ref, bf16[512,1280]{1,0:T(8,128)(2,1)} %get-tuple-element.17.up_ref, ...), custom_call_target="tpu_custom_call" | custom-call | tf_op jit(solution)/shard_map/layer0/pallas_call | solution.py:456
  142.4 0.0 copy-start
  142.4 89.8 %layer1.1 = (bf16[8,128,1280]{2,1,0:T(8,128)(2,1)}, bf16[1,8,128]{2,1,0:T(8,128)(2,1)}, bf16[128,2048]{1,0:T(8,128)(2,1)}) custom-call(bf16[8,128,512]{2,1,0:T(8,128)(2,1)} %get-tuple-element.20.x_ref, f32[1,512]{1,0:T(1,128)} %get-tuple-element.21.gain_ref, bf16[512,1280]{1,0:T(8,128)(2,1)} %get-tuple-element.22.up_ref, ...), custom_call_target="tpu_custom_call" | custom-call | tf_op jit(solution)/shard_map/layer1/pallas_call | solution.py:456
  232.2 0.0 copy-done
  232.2 0.0 copy-start.1
  232.2 0.0 copy-start.2
  232.3 2.2 broadcast_select_fusion.1
  234.4 0.1 collective-permute-start
  234.5 0.0 copy-done.1
  234.5 0.0 copy-done.2
  234.5 0.9 select_bitcast_fusion
  235.4 4.0 %collective-permute-done = bf16[1024,1280]{1,0:T(8,128)(2,1)S(1)} collective-permute-done((bf16[1024,1280]{1,0:T(8,128)(2,1)S(1)}, bf16[1024,1280]{1,0:T(8,128)(2,1)S(1)}, u32[]{:S(2)}, u32[]{:S(2)}) %collective-permute-start) | collective-permute-done | bytes 2621472 | tf_op jit(solution)/shard_map/ppermute | solution.py:826
  239.4 0.0 copy-start.3
  239.4 0.5 bitcast_select_fusion.1
  239.9 0.7 copy-done.3
  240.6 4.2 %fusion.7 = bf16[1,2560,512]{2,1,0:T(8,128)(2,1)} fusion(bf16[1024,512]{1,0:T(8,128)(2,1)S(1)} %bitcast.11, bf16[1024,1280]{1,0:T(8,128)(2,1)S(1)} %get-tuple-element.29, bf16[1024,1280]{1,0:T(8,128)(2,1)S(1)} %get-tuple-element.28), kind=kOutput, calls=%fused_computation.5 | convolution fusion | flops 2696151040 | bytes 8912896 | tf_op jit(solution)/shard_map/dot_general | solution.py:849
Async XLA Ops:
  142.4 89.8 %copy-start = (bf16[8,128,1280]{2,1,0:T(8,128)(2,1)S(1)}, bf16[8,128,1280]{2,1,0:T(8,128)(2,1)}, u32[]{:S(2)}) copy-start(bf16[8,128,1280]{2,1,0:T(8,128)(2,1)} %get-tuple-element.25) | copy-start | bytes 7864324
  232.2 2.3 copy-start.1
  232.2 2.3 copy-start.2
  234.4 5.0 %collective-permute-start = (bf16[1024,1280]{1,0:T(8,128)(2,1)S(1)}, bf16[1024,1280]{1,0:T(8,128)(2,1)S(1)}, u32[]{:S(2)}, u32[]{:S(2)}) collective-permute-start(bf16[1024,1280]{1,0:T(8,128)(2,1)S(1)} %bitcast.10), channel_id=1, source_target_pairs={{0,16},{16,0},{1,17},{17,1},{2,18},{18,2},{3,19},{19,3},{4,20},{20... | collective-permute-start | bytes 7864328 | tf_op jit(solution)/shard_map/ppermute | solution.py:826
  239.4 1.2 copy-start.3

commit v5 on v4

--- a/solution.py
+++ b/solution.py
@@ -510,6 +510,7 @@
     cot_buf,
     tok_ss,
     tok_rs,
+    ty_ss,
     tf_ss,
     tf_rs,
     cot_ss,
@@ -550,14 +551,7 @@
         greet(place(lax.rem(member + off, group)))
     feature_home = me // per_tensor
     at_home = feature_home == tensor
-    for source in range(dp_count):
-
-        @pl.when(jnp.logical_not(at_home & (me == source)))
-        def _():
-            greet({"dp": source, "tensor": feature_home})
-
-    self_send = at_home.astype(jnp.int32)
-    pl.semaphore_wait(barrier, dp_count - 1 + group - 1 + per_tensor * tensors - self_send)
+    pl.semaphore_wait(barrier, dp_count - 1 + group - 1)
 
     my_half = pl.ds(pl.multiple_of(core * half_rows, half_rows), half_rows)
     my_part = pl.ds(pl.multiple_of(tensor * part_rows, part_rows), part_rows)
@@ -565,13 +559,13 @@
     def columns(index, size):
         return pl.ds(pl.multiple_of(index * size, size), size)
 
-    def token_copy(q, tt):
+    def token_copy(q):
         return remote(
             tok_ref.at[my_half, pl.ds(q * slice_width, slice_width)],
             x_buf.at[me, my_half],
-            tok_ss.at[q * tensors + tt],
+            tok_ss.at[q],
             tok_rs.at[me],
-            {"dp": tensor * per_tensor + q, "tensor": tt},
+            {"dp": tensor * per_tensor + q},
         )
 
     def token_local(q):
@@ -581,20 +575,27 @@
             tok_rs.at[me],
         )
 
-    def is_self(q, tt):
-        return (tensor * per_tensor + q == me) & (tensor == tt)
+    def is_self(q):
+        return tensor * per_tensor + q == me
+
+    def token_share(source, off):
+        return remote(
+            x_buf.at[source, my_half],
+            x_buf.at[source, my_half],
+            ty_ss.at[source * tensors + off],
+            tok_rs.at[source],
+            {"tensor": lax.rem(tensor + off, tensors)},
+        )
 
     for q in range(per_tensor):
-        for tt in range(tensors):
-            local = is_self(q, tt)
-
-            @pl.when(local)
-            def _():
-                token_local(q).start()
-
-            @pl.when(jnp.logical_not(local))
-            def _():
-                token_copy(q, tt).start()
+
+        @pl.when(is_self(q))
+        def _():
+            token_local(q).start()
+
+        @pl.when(jnp.logical_not(is_self(q)))
+        def _():
+            token_copy(q).start()
 
     def gain_copy(off):
         return remote(
@@ -674,11 +675,16 @@
             {"section": other},
         )
 
-    their_half = columns(other, half_rows)
     for source in range(dp_count):
         pltpu.make_async_copy(
             x_buf.at[source, my_half], x_buf.at[source, my_half], tok_rs.at[source]
         ).wait()
+
+        @pl.when(at_home)
+        def _():
+            for off in range(1, tensors):
+                token_share(source, off).start()
+
         token_forward(source).start()
 
     ends = []
@@ -730,16 +736,18 @@
     put(cot_buf, cot_out)
 
     for q in range(per_tensor):
-        for tt in range(tensors):
-
-            @pl.when(jnp.logical_not(is_self(q, tt)))
-            def _():
-                token_copy(q, tt).wait_send()
+
+        @pl.when(jnp.logical_not(is_self(q)))
+        def _():
+            token_copy(q).wait_send()
 
     @pl.when(at_home)
     def _():
         for off in range(1, group):
             gain_copy(off).wait_send()
+        for source in range(dp_count):
+            for off in range(1, tensors):
+                token_share(source, off).wait_send()
 
     give_up.wait_send()
     give_down.wait_send()
@@ -794,6 +802,7 @@
             pltpu.VMEM((dp_count, rows, slice_width), BF16),
             dma((dp_count,)),
             dma((dp_count,)),
+            dma((dp_count * tensors,)),
             dma((dp_count,)),
             dma((dp_count,)),
             dma((dp_count,)),

time: 249 us -> 245 us (0.984)
  Pallas kernels: 230 us -> 226 us
    pallas_call x1, Pallas kernels: 45.1 us -> 39.2 us  [front(): pl.pallas_call(functools.partial(front_kernel, sizes), name='front', out_...]
where the time goes in v5:
time: 245 us; the launch traced here: 241 us
  Pallas kernels  226 us (92%)
  other arithmetic  4.83 us (2%)
  matrix products  4.25 us (2%)
  waiting for transfers between devices  4.02 us (2%)
    pallas_call x2, Pallas kernels, layer_step(): pl.pallas_call(functools.partial(layer_kernel, sizes, inner, width, layer...  187 us
    pallas_call x1, Pallas kernels, front(): pl.pallas_call(functools.partial(front_kernel, sizes), name='front', out_...  39.2 us
  transfers between devices with their start and end apart: 1, of which 1 were waited for; matrix products, arithmetic and copies ran while one was open for 0% of the time, Pallas kernels for 0%

profile of v5, /device:TPU:0, one launch (start us, length us, event | category | flops | bytes accessed | tf_op | source)
XLA Modules:
  0.0 240.7 jit_solution(6375043114817033402)
XLA Ops:
  0.6 1.3 convert_element_type.6.gain_ref
  1.9 39.2 %front.1 = (bf16[8,128,512]{2,1,0:T(8,128)(2,1)}, f32[1,512]{1,0:T(1,128)}, f32[1,512]{1,0:T(1,128)}, bf16[512,1280]{1,0:T(8,128)(2,1)}, bf16[512,1280]{1,0:T(8,...) custom-call(bf16[128,2048]{1,0:T(8,128)(2,1)} %tok_ref.1, ...), custom_call_target="tpu_custom_call" | custom-call | tf_op jit(solution)/shard_map/front/pallas_call | solution.py:782
  41.2 93.4 %layer0.1 = (bf16[8,128,1280]{2,1,0:T(8,128)(2,1)}, bf16[8,128,512]{2,1,0:T(8,128)(2,1)}, bf16[128,2048]{1,0:T(8,128)(2,1)}) custom-call(bf16[8,128,512]{2,1,0:T(8,128)(2,1)} %get-tuple-element.15.x_ref, f32[1,512]{1,0:T(1,128)} %get-tuple-element.16.gain_ref, bf16[512,1280]{1,0:T(8,128)(2,1)} %get-tuple-element.17.up_ref, ...), custom_call_target="tpu_custom_call" | custom-call | tf_op jit(solution)/shard_map/layer0/pallas_call | solution.py:456
  134.5 0.0 copy-start
  134.6 93.5 %layer1.1 = (bf16[8,128,1280]{2,1,0:T(8,128)(2,1)}, bf16[1,8,128]{2,1,0:T(8,128)(2,1)}, bf16[128,2048]{1,0:T(8,128)(2,1)}) custom-call(bf16[8,128,512]{2,1,0:T(8,128)(2,1)} %get-tuple-element.20.x_ref, f32[1,512]{1,0:T(1,128)} %get-tuple-element.21.gain_ref, bf16[512,1280]{1,0:T(8,128)(2,1)} %get-tuple-element.22.up_ref, ...), custom_call_target="tpu_custom_call" | custom-call | tf_op jit(solution)/shard_map/layer1/pallas_call | solution.py:456
  228.1 0.0 copy-done
  228.1 0.0 copy-start.1
  228.1 0.0 copy-start.2
  228.1 2.2 broadcast_select_fusion.1
  230.3 0.1 collective-permute-start
  230.4 0.0 copy-done.1
  230.4 0.0 copy-done.2
  230.4 0.9 select_bitcast_fusion
  231.2 4.0 %collective-permute-done = bf16[1024,1280]{1,0:T(8,128)(2,1)S(1)} collective-permute-done((bf16[1024,1280]{1,0:T(8,128)(2,1)S(1)}, bf16[1024,1280]{1,0:T(8,128)(2,1)S(1)}, u32[]{:S(2)}, u32[]{:S(2)}) %collective-permute-start) | collective-permute-done | bytes 2621472 | tf_op jit(solution)/shard_map/ppermute | solution.py:835
  235.3 0.0 copy-start.3
  235.3 0.5 bitcast_select_fusion.1
  235.8 0.7 copy-done.3
  236.5 4.2 %fusion.7 = bf16[1,2560,512]{2,1,0:T(8,128)(2,1)} fusion(bf16[1024,512]{1,0:T(8,128)(2,1)S(1)} %bitcast.11, bf16[1024,1280]{1,0:T(8,128)(2,1)S(1)} %get-tuple-element.29, bf16[1024,1280]{1,0:T(8,128)(2,1)S(1)} %get-tuple-element.28), kind=kOutput, calls=%fused_computation.5 | convolution fusion | flops 2696151040 | bytes 8912896 | tf_op jit(solution)/shard_map/dot_general | solution.py:858
Async XLA Ops:
  134.5 93.5 %copy-start = (bf16[8,128,1280]{2,1,0:T(8,128)(2,1)S(1)}, bf16[8,128,1280]{2,1,0:T(8,128)(2,1)}, u32[]{:S(2)}) copy-start(bf16[8,128,1280]{2,1,0:T(8,128)(2,1)} %get-tuple-element.25) | copy-start | bytes 7864324
  228.1 2.3 copy-start.1
  228.1 2.3 copy-start.2
  230.3 5.0 %collective-permute-start = (bf16[1024,1280]{1,0:T(8,128)(2,1)S(1)}, bf16[1024,1280]{1,0:T(8,128)(2,1)S(1)}, u32[]{:S(2)}, u32[]{:S(2)}) collective-permute-start(bf16[1024,1280]{1,0:T(8,128)(2,1)S(1)} %bitcast.10), channel_id=1, source_target_pairs={{0,16},{16,0},{1,17},{17,1},{2,18},{18,2},{3,19},{19,3},{4,20},{20... | collective-permute-start | bytes 7864328 | tf_op jit(solution)/shard_map/ppermute | solution.py:835
  235.3 1.2 copy-start.3
